TPU v7x, 32 devices: a whole 2x2x4 slice. The times are simulated.
32 devices in a mesh: dp: 2 (over x), tp: 16 (over y, z, core).
Axes of the slice: x: 2, y: 2, z: 4, core: 2. Of those that a mesh axis runs over, the one named last changes fastest.
Arguments:
- x: bfloat16 [5120, 7168], P(('dp', 'tp')), parts along dimension 0
- dy: bfloat16 [5120, 7168], P(('dp', 'tp')), parts along dimension 0
- pre: bfloat16 [5120, 28672], P('dp', 'tp'), parts along dimension 0
- w_in: bfloat16 [7168, 28672], P(None, 'tp')
- w_down: bfloat16 [28672, 7168], P('tp')
Outputs:
- output 1: bfloat16 [5120, 7168], P(('dp', 'tp')), parts along dimension 0
- output 2: bfloat16 [14336, 28672], P('dp', 'tp'), parts along dimension 0
- output 3: bfloat16 [57344, 7168], P(('dp', 'tp')), parts along dimension 0
There are 2 independent parts. A program takes and returns all parts, laid end to end along the dimension named above; an argument that names none is the same for every part.
All inputs are finite; a program needn't handle non-finite values.
Results may differ from a plain program's by a relative error of at most 0.012.
Values are sent between devices in bfloat16 or wider.
A program may use at most 2 GiB of HBM per device.

v0:
```python
import jax
import jax.numpy as jnp


def act(pre):
    return jax.nn.gelu(pre)


def solution(mesh):
    def step(x, dy, pre, w_in, w_down):
        hidden, back = jax.vjp(act, pre.astype(jnp.float32))
        d_hidden = jnp.dot(dy, w_down.T, preferred_element_type=jnp.float32)
        d_pre = back(d_hidden)[0].astype(jnp.bfloat16)
        dx = jnp.dot(d_pre, w_in.T)
        groups = mesh.shape["dp"]

        def by_group(a, b):
            a, b = (t.reshape(groups, -1, t.shape[-1]) for t in (a, b))
            product = jnp.einsum("gta,gtb->gab", a, b, preferred_element_type=jnp.float32)
            return product.astype(jnp.bfloat16).reshape(-1, b.shape[-1])

        return dx, by_group(x, d_pre), by_group(hidden.astype(jnp.bfloat16), dy)

    return step
```

profile of v0, /device:TPU:0, one launch (start us, length us, event | category | flops | bytes accessed | tf_op | source)
XLA Modules:
  0.0 1566.8 jit_solution(11147530424004995825)
XLA Ops:
  17.0 226.8 %all-gather.5.cloned.1.call-done = bf16[2560,7168]{1,0:T(8,128)(2,1)} async-done(((bf16[160,7168]{1,0:T(8,128)(2,1)}), bf16[2560,7168]{1,0:T(8,128)(2,1)}) %all-gather.5.cloned.1.call-update) | async-done | bytes 36700176 | tf_op args[1]
  243.9 90.9 %fusion.40 = (bf16[1,2560,1792]{2,1,0:T(8,128)(2,1)}, bf16[2560,1792]{1,0:T(8,128)(2,1)}) fusion(bf16[2560,1792]{1,0:T(8,128)(2,1)} %param.6, bf16[2560,7168]{1,0:T(8,128)(2,1)} %all-gather.5.cloned.1.call-done, bf16[1792,7168]{1,0:T(8,128)(2,1)} %param.5), kind=kOutput, calls=%fused_computation.59 | convolution fusion | flops 65872199680 | bytes 89915392 | tf_op jit(solution)/dot_general | solution.py:12
  334.7 75.5 %fusion.41 = bf16[2560,7168]{1,0:T(8,128)(2,1)} fusion(bf16[2560,1792]{1,0:T(8,128)(2,1)} %get-tuple-element.71, bf16[7168,1792]{1,0:T(8,128)(2,1)} %param.7), kind=kOutput, calls=%fused_computation.60 | convolution fusion | flops 65766686720 | bytes 71565312 | tf_op jit(solution)/dot_general | solution.py:14
  410.9 650.8 %while.4 = (bf16[1,2560,1792]{2,1,0:T(8,128)(2,1)}, bf16[1,1,160,7168]{3,2,1,0:T(8,128)(2,1)}, f32[1,1792,7168]{2,1,0:T(8,128)}, bf16[1,1,160,7168]{3,2,1,0:T(8,...) while((bf16[1,2560,1792]{2,1,0:T(8,128)(2,1)}, ...), condition=%wide.windowed_dot_general_cond_ag.clone, body=%wide.windowed_dot_general_body_ag.clone.sunk | while | flops 16489381888 | bytes 269746752 | solution.py:19
  416.1 25.7 %fusion.57 = f32[1792,7168,1]{1,0,2:T(8,128)} fusion(bf16[1,1,160,7168]{3,2,1,0:T(8,128)(2,1)} %get-tuple-element.148, bf16[1,1,160,7168]{3,2,1,0:T(8,128)(2,1)} %get-tuple-element.146, s32[]{:T(128)S(6)} %multiply.30, bf16[1,1,2560,1792]{3,2,1,0:T(8,128)(2,1)} %bitcast.106, s32[]{:T(128)S(6)} %multiply.31), kind=kOutput, calls=%fused_computation.7.clone.1 | convolution fusion | flops 8225423360 | bytes 65142792 | tf_op jit(solution)/gta,gtb->gab/dot_general | solution.py:19
  441.8 20.9 %collective-permute-done = bf16[1,1,160,7168]{3,2,1,0:T(8,128)(2,1)S(1)} collective-permute-done((bf16[1,1,160,7168]{3,2,1,0:T(8,128)(2,1)}, bf16[1,1,160,7168]{3,2,1,0:T(8,128)(2,1)S(1)}, u32[]{:S(2)}, u32[]{:S(2)}) %collective-permute-start) | collective-permute-done | bytes 2293792 | tf_op jit(solution)/gta,gtb->gab/dot_general | solution.py:19
  467.3 40.1 %bitcast_add_fusion.6 = f32[1,1792,7168]{2,1,0:T(8,128)} fusion(f32[1792,7168,1]{1,0,2:T(8,128)} %fusion.57, f32[1,1792,7168]{2,1,0:T(8,128)} %get-tuple-element.147, pred[]{:T(512)S(6)} %compare.12, bf16[1,1,160,7168]{3,2,1,0:T(8,128)(2,1)} %collective-permute-done.2, bf16[1,1,160,7168]{3,2,1,0:T(8,128)(2,1)S(1)} %collective-permute-done, ...), kind=kOutput, calls=%fused_computation.clone.3 | convolution fusion | flops 8263958528 | bytes 167903248 | tf_op jit(solution)/gta,gtb->gab/dot_general | solution.py:19
  507.4 54.6 %collective-permute-done.1 = bf16[1,1,160,7168]{3,2,1,0:T(8,128)(2,1)} collective-permute-done((bf16[1,1,160,7168]{3,2,1,0:T(8,128)(2,1)S(1)}, bf16[1,1,160,7168]{3,2,1,0:T(8,128)(2,1)}, u32[]{:S(2)}, u32[]{:S(2)}) %collective-permute-start.1) | collective-permute-done | bytes 2293792 | tf_op jit(solution)/gta,gtb->gab/dot_general | solution.py:19
  584.6 25.7 %fusion.57 = f32[1792,7168,1]{1,0,2:T(8,128)} fusion(bf16[1,1,160,7168]{3,2,1,0:T(8,128)(2,1)} %get-tuple-element.148, bf16[1,1,160,7168]{3,2,1,0:T(8,128)(2,1)} %get-tuple-element.146, s32[]{:T(128)S(6)} %multiply.30, bf16[1,1,2560,1792]{3,2,1,0:T(8,128)(2,1)} %bitcast.106, s32[]{:T(128)S(6)} %multiply.31), kind=kOutput, calls=%fused_computation.7.clone.1 | convolution fusion | flops 8225423360 | bytes 65142792 | tf_op jit(solution)/gta,gtb->gab/dot_general | solution.py:19
  610.3 50.3 %collective-permute-done = bf16[1,1,160,7168]{3,2,1,0:T(8,128)(2,1)S(1)} collective-permute-done((bf16[1,1,160,7168]{3,2,1,0:T(8,128)(2,1)}, bf16[1,1,160,7168]{3,2,1,0:T(8,128)(2,1)S(1)}, u32[]{:S(2)}, u32[]{:S(2)}) %collective-permute-start) | collective-permute-done | bytes 2293792 | tf_op jit(solution)/gta,gtb->gab/dot_general | solution.py:19
  665.2 31.8 %collective-permute-done.2 = bf16[1,1,160,7168]{3,2,1,0:T(8,128)(2,1)} collective-permute-done((bf16[1,1,160,7168]{3,2,1,0:T(8,128)(2,1)}, bf16[1,1,160,7168]{3,2,1,0:T(8,128)(2,1)}, u32[]{:S(2)}, u32[]{:S(2)}) %collective-permute-start.2) | collective-permute-done | bytes 2293792 | tf_op jit(solution)/gta,gtb->gab/dot_general | solution.py:19
  696.9 52.6 %bitcast_add_fusion.6 = f32[1,1792,7168]{2,1,0:T(8,128)} fusion(f32[1792,7168,1]{1,0,2:T(8,128)} %fusion.57, f32[1,1792,7168]{2,1,0:T(8,128)} %get-tuple-element.147, pred[]{:T(512)S(6)} %compare.12, bf16[1,1,160,7168]{3,2,1,0:T(8,128)(2,1)} %collective-permute-done.2, bf16[1,1,160,7168]{3,2,1,0:T(8,128)(2,1)S(1)} %collective-permute-done, ...), kind=kOutput, calls=%fused_computation.clone.3 | convolution fusion | flops 8263958528 | bytes 167903248 | tf_op jit(solution)/gta,gtb->gab/dot_general | solution.py:19
  767.3 25.7 %fusion.57 = f32[1792,7168,1]{1,0,2:T(8,128)} fusion(bf16[1,1,160,7168]{3,2,1,0:T(8,128)(2,1)} %get-tuple-element.148, bf16[1,1,160,7168]{3,2,1,0:T(8,128)(2,1)} %get-tuple-element.146, s32[]{:T(128)S(6)} %multiply.30, bf16[1,1,2560,1792]{3,2,1,0:T(8,128)(2,1)} %bitcast.106, s32[]{:T(128)S(6)} %multiply.31), kind=kOutput, calls=%fused_computation.7.clone.1 | convolution fusion | flops 8225423360 | bytes 65142792 | tf_op jit(solution)/gta,gtb->gab/dot_general | solution.py:19
  792.9 21.1 %collective-permute-done = bf16[1,1,160,7168]{3,2,1,0:T(8,128)(2,1)S(1)} collective-permute-done((bf16[1,1,160,7168]{3,2,1,0:T(8,128)(2,1)}, bf16[1,1,160,7168]{3,2,1,0:T(8,128)(2,1)S(1)}, u32[]{:S(2)}, u32[]{:S(2)}) %collective-permute-start) | collective-permute-done | bytes 2293792 | tf_op jit(solution)/gta,gtb->gab/dot_general | solution.py:19
  832.2 52.6 %bitcast_add_fusion.6 = f32[1,1792,7168]{2,1,0:T(8,128)} fusion(f32[1792,7168,1]{1,0,2:T(8,128)} %fusion.57, f32[1,1792,7168]{2,1,0:T(8,128)} %get-tuple-element.147, pred[]{:T(512)S(6)} %compare.12, bf16[1,1,160,7168]{3,2,1,0:T(8,128)(2,1)} %collective-permute-done.2, bf16[1,1,160,7168]{3,2,1,0:T(8,128)(2,1)S(1)} %collective-permute-done, ...), kind=kOutput, calls=%fused_computation.clone.3 | convolution fusion | flops 8263958528 | bytes 167903248 | tf_op jit(solution)/gta,gtb->gab/dot_general | solution.py:19
  895.3 33.3 %collective-permute-done.3 = bf16[1,1,160,7168]{3,2,1,0:T(8,128)(2,1)} collective-permute-done((bf16[1,1,160,7168]{3,2,1,0:T(8,128)(2,1)}, bf16[1,1,160,7168]{3,2,1,0:T(8,128)(2,1)}, u32[]{:S(2)}, u32[]{:S(2)}) %collective-permute-start.3) | collective-permute-done | bytes 2293792 | tf_op jit(solution)/gta,gtb->gab/dot_general | solution.py:19
  931.8 25.7 %fusion.57 = f32[1792,7168,1]{1,0,2:T(8,128)} fusion(bf16[1,1,160,7168]{3,2,1,0:T(8,128)(2,1)} %get-tuple-element.148, bf16[1,1,160,7168]{3,2,1,0:T(8,128)(2,1)} %get-tuple-element.146, s32[]{:T(128)S(6)} %multiply.30, bf16[1,1,2560,1792]{3,2,1,0:T(8,128)(2,1)} %bitcast.106, s32[]{:T(128)S(6)} %multiply.31), kind=kOutput, calls=%fused_computation.7.clone.1 | convolution fusion | flops 8225423360 | bytes 65142792 | tf_op jit(solution)/gta,gtb->gab/dot_general | solution.py:19
  957.5 31.5 %collective-permute-done = bf16[1,1,160,7168]{3,2,1,0:T(8,128)(2,1)S(1)} collective-permute-done((bf16[1,1,160,7168]{3,2,1,0:T(8,128)(2,1)}, bf16[1,1,160,7168]{3,2,1,0:T(8,128)(2,1)S(1)}, u32[]{:S(2)}, u32[]{:S(2)}) %collective-permute-start) | collective-permute-done | bytes 2293792 | tf_op jit(solution)/gta,gtb->gab/dot_general | solution.py:19
  1009.1 52.6 %bitcast_add_fusion.6 = f32[1,1792,7168]{2,1,0:T(8,128)} fusion(f32[1792,7168,1]{1,0,2:T(8,128)} %fusion.57, f32[1,1792,7168]{2,1,0:T(8,128)} %get-tuple-element.147, pred[]{:T(512)S(6)} %compare.12, bf16[1,1,160,7168]{3,2,1,0:T(8,128)(2,1)} %collective-permute-done.2, bf16[1,1,160,7168]{3,2,1,0:T(8,128)(2,1)S(1)} %collective-permute-done, ...), kind=kOutput, calls=%fused_computation.clone.3 | convolution fusion | flops 8263958528 | bytes 167903248 | tf_op jit(solution)/gta,gtb->gab/dot_general | solution.py:19
  1061.7 40.4 %copy = bf16[1,1792,7168]{1,2,0:T(8,128)(2,1)} copy(f32[1,1792,7168]{2,1,0:T(8,128)} %get-tuple-element.12) | data formatting | bytes 77070336 | tf_op jit(solution)/gta,gtb->gab/dot_general | solution.py:19
  1102.1 431.7 %while.5 = (bf16[1,2560,1792]{2,1,0:T(8,128)(2,1)}, bf16[1,1,160,7168]{3,2,1,0:T(8,128)(2,1)}, f32[1,1792,7168]{2,1,0:T(8,128)}, bf16[1,1,160,7168]{3,2,1,0:T(8,...) while((bf16[1,2560,1792]{2,1,0:T(8,128)(2,1)}, ...), condition=%wide.windowed_dot_general_cond_ag.1.clone, body=%wide.windowed_dot_general_body_ag.1.clone.sunk | while | flops 16489381888 | bytes 278921792 | solution.py:19
  1109.0 25.7 %fusion.60 = f32[1792,7168,1]{1,0,2:T(8,128)} fusion(bf16[1,1,160,7168]{3,2,1,0:T(8,128)(2,1)} %get-tuple-element.181, bf16[1,1,160,7168]{3,2,1,0:T(8,128)(2,1)} %get-tuple-element.179, s32[]{:T(128)S(6)} %multiply.34, bf16[1,1,2560,1792]{3,2,1,0:T(8,128)(2,1)} %bitcast.103, s32[]{:T(128)S(6)} %multiply.35), kind=kOutput, calls=%fused_computation.28.clone.1 | convolution fusion | flops 8225423360 | bytes 65142792 | tf_op jit(solution)/gta,gtb->gab/dot_general | solution.py:19
  1158.3 40.0 %bitcast_add_fusion.7 = f32[1,1792,7168]{2,1,0:T(8,128)} fusion(f32[1792,7168,1]{1,0,2:T(8,128)} %fusion.60, f32[1,1792,7168]{2,1,0:T(8,128)} %get-tuple-element.180, pred[]{:T(512)S(6)} %compare.13, bf16[1,1,160,7168]{3,2,1,0:T(8,128)(2,1)} %collective-permute-done.6, bf16[1,1,160,7168]{3,2,1,0:T(8,128)(2,1)S(1)} %collective-permute-done.4, ...), kind=kOutput, calls=%fused_computation.21.clone.1 | convolution fusion | flops 8263958528 | bytes 167903248 | tf_op jit(solution)/gta,gtb->gab/dot_general | solution.py:19
  1210.7 25.7 %fusion.60 = f32[1792,7168,1]{1,0,2:T(8,128)} fusion(bf16[1,1,160,7168]{3,2,1,0:T(8,128)(2,1)} %get-tuple-element.181, bf16[1,1,160,7168]{3,2,1,0:T(8,128)(2,1)} %get-tuple-element.179, s32[]{:T(128)S(6)} %multiply.34, bf16[1,1,2560,1792]{3,2,1,0:T(8,128)(2,1)} %bitcast.103, s32[]{:T(128)S(6)} %multiply.35), kind=kOutput, calls=%fused_computation.28.clone.1 | convolution fusion | flops 8225423360 | bytes 65142792 | tf_op jit(solution)/gta,gtb->gab/dot_general | solution.py:19
  1236.4 19.1 %collective-permute-done.4 = bf16[1,1,160,7168]{3,2,1,0:T(8,128)(2,1)S(1)} collective-permute-done((bf16[1,1,160,7168]{3,2,1,0:T(8,128)(2,1)}, bf16[1,1,160,7168]{3,2,1,0:T(8,128)(2,1)S(1)}, u32[]{:S(2)}, u32[]{:S(2)}) %collective-permute-start.4) | collective-permute-done | bytes 2293792 | tf_op jit(solution)/gta,gtb->gab/dot_general | solution.py:19
  1260.2 52.5 %bitcast_add_fusion.7 = f32[1,1792,7168]{2,1,0:T(8,128)} fusion(f32[1792,7168,1]{1,0,2:T(8,128)} %fusion.60, f32[1,1792,7168]{2,1,0:T(8,128)} %get-tuple-element.180, pred[]{:T(512)S(6)} %compare.13, bf16[1,1,160,7168]{3,2,1,0:T(8,128)(2,1)} %collective-permute-done.6, bf16[1,1,160,7168]{3,2,1,0:T(8,128)(2,1)S(1)} %collective-permute-done.4, ...), kind=kOutput, calls=%fused_computation.21.clone.1 | convolution fusion | flops 8263958528 | bytes 167903248 | tf_op jit(solution)/gta,gtb->gab/dot_general | solution.py:19
  1320.7 25.7 %fusion.60 = f32[1792,7168,1]{1,0,2:T(8,128)} fusion(bf16[1,1,160,7168]{3,2,1,0:T(8,128)(2,1)} %get-tuple-element.181, bf16[1,1,160,7168]{3,2,1,0:T(8,128)(2,1)} %get-tuple-element.179, s32[]{:T(128)S(6)} %multiply.34, bf16[1,1,2560,1792]{3,2,1,0:T(8,128)(2,1)} %bitcast.103, s32[]{:T(128)S(6)} %multiply.35), kind=kOutput, calls=%fused_computation.28.clone.1 | convolution fusion | flops 8225423360 | bytes 65142792 | tf_op jit(solution)/gta,gtb->gab/dot_general | solution.py:19
  1346.4 17.8 %collective-permute-done.4 = bf16[1,1,160,7168]{3,2,1,0:T(8,128)(2,1)S(1)} collective-permute-done((bf16[1,1,160,7168]{3,2,1,0:T(8,128)(2,1)}, bf16[1,1,160,7168]{3,2,1,0:T(8,128)(2,1)S(1)}, u32[]{:S(2)}, u32[]{:S(2)}) %collective-permute-start.4) | collective-permute-done | bytes 2293792 | tf_op jit(solution)/gta,gtb->gab/dot_general | solution.py:19
  1370.0 52.5 %bitcast_add_fusion.7 = f32[1,1792,7168]{2,1,0:T(8,128)} fusion(f32[1792,7168,1]{1,0,2:T(8,128)} %fusion.60, f32[1,1792,7168]{2,1,0:T(8,128)} %get-tuple-element.180, pred[]{:T(512)S(6)} %compare.13, bf16[1,1,160,7168]{3,2,1,0:T(8,128)(2,1)} %collective-permute-done.6, bf16[1,1,160,7168]{3,2,1,0:T(8,128)(2,1)S(1)} %collective-permute-done.4, ...), kind=kOutput, calls=%fused_computation.21.clone.1 | convolution fusion | flops 8263958528 | bytes 167903248 | tf_op jit(solution)/gta,gtb->gab/dot_general | solution.py:19
  1430.6 25.7 %fusion.60 = f32[1792,7168,1]{1,0,2:T(8,128)} fusion(bf16[1,1,160,7168]{3,2,1,0:T(8,128)(2,1)} %get-tuple-element.181, bf16[1,1,160,7168]{3,2,1,0:T(8,128)(2,1)} %get-tuple-element.179, s32[]{:T(128)S(6)} %multiply.34, bf16[1,1,2560,1792]{3,2,1,0:T(8,128)(2,1)} %bitcast.103, s32[]{:T(128)S(6)} %multiply.35), kind=kOutput, calls=%fused_computation.28.clone.1 | convolution fusion | flops 8225423360 | bytes 65142792 | tf_op jit(solution)/gta,gtb->gab/dot_general | solution.py:19
  1479.8 52.5 %bitcast_add_fusion.7 = f32[1,1792,7168]{2,1,0:T(8,128)} fusion(f32[1792,7168,1]{1,0,2:T(8,128)} %fusion.60, f32[1,1792,7168]{2,1,0:T(8,128)} %get-tuple-element.180, pred[]{:T(512)S(6)} %compare.13, bf16[1,1,160,7168]{3,2,1,0:T(8,128)(2,1)} %collective-permute-done.6, bf16[1,1,160,7168]{3,2,1,0:T(8,128)(2,1)S(1)} %collective-permute-done.4, ...), kind=kOutput, calls=%fused_computation.21.clone.1 | convolution fusion | flops 8263958528 | bytes 167903248 | tf_op jit(solution)/gta,gtb->gab/dot_general | solution.py:19
  1533.8 25.8 %convert_bitcast_fusion = bf16[1792,7168]{1,0:T(8,128)(2,1)} fusion(f32[1,1792,7168]{2,1,0:T(8,128)} %get-tuple-element.13), kind=kLoop, calls=%fused_computation.48 | loop fusion | flops 12845056 | bytes 77070336 | tf_op jit(solution)/reshape | solution.py:20
  (86 shorter events, 196.6 us)
Async XLA Ops:
  7.2 236.7 %all-gather.5.cloned.1.call-start = ((), (), s32[]{:S(2)}) async-start(), calls=%async_computation.1 | async-start | bytes 38993920 | tf_op args[1]
  13.7 1545.9 %reduce-scatter.4.cloned.1.call-start = ((), (), s32[]{:S(2)}) async-start(), calls=%async_computation.2 | async-start | bytes 38993920
  13.7 1088.3 %collective-permute-start.9 = (bf16[1,1,160,7168]{3,2,1,0:T(8,128)(2,1)}, bf16[1,1,160,7168]{3,2,1,0:T(8,128)(2,1)}, u32[]{:S(2)}, u32[]{:S(2)}) collective-permute-start(bf16[1,1,160,7168]{3,2,1,0:T(8,128)(2,1)} %bitcast.109), channel_id=11, source_target_pairs={{0,1},{1,2},{2,3},{3,4},{4,5},{5,6},{6,7},{7,8},{8,9},{9,10},{10,1... | collective-permute-start | bytes 6881288 | tf_op jit(solution)/gta,gtb->gab/dot_general | solution.py:19
  14.3 395.9 %collective-permute-start.8 = (bf16[1,1,160,7168]{3,2,1,0:T(8,128)(2,1)}, bf16[1,1,160,7168]{3,2,1,0:T(8,128)(2,1)}, u32[]{:S(2)}, u32[]{:S(2)}) collective-permute-start(bf16[1,1,160,7168]{3,2,1,0:T(8,128)(2,1)} %bitcast.2), channel_id=5, source_target_pairs={{0,1},{1,2},{2,3},{3,4},{4,5},{5,6},{6,7},{7,8},{8,9},{9,10},{10,1... | collective-permute-start | bytes 6881288 | tf_op jit(solution)/gta,gtb->gab/dot_general | solution.py:19
  411.1 51.6 %collective-permute-start = (bf16[1,1,160,7168]{3,2,1,0:T(8,128)(2,1)}, bf16[1,1,160,7168]{3,2,1,0:T(8,128)(2,1)S(1)}, u32[]{:S(2)}, u32[]{:S(2)}) collective-permute-start(bf16[1,1,160,7168]{3,2,1,0:T(8,128)(2,1)} %get-tuple-element.146), channel_id=6, source_target_pairs={{0,15},{1,0},{2,1},{3,2},{4,3},{5,4},{6,5},{7,6},{8,7},{9,8},{10,9... | collective-permute-start | bytes 6881288 | tf_op jit(solution)/gta,gtb->gab/dot_general | solution.py:19
  413.4 53.9 %collective-permute-start.2 = (bf16[1,1,160,7168]{3,2,1,0:T(8,128)(2,1)}, bf16[1,1,160,7168]{3,2,1,0:T(8,128)(2,1)}, u32[]{:S(2)}, u32[]{:S(2)}) collective-permute-start(bf16[1,1,160,7168]{3,2,1,0:T(8,128)(2,1)} %get-tuple-element.148), channel_id=7, source_target_pairs={{0,1},{1,2},{2,3},{3,4},{4,5},{5,6},{6,7},{7,8},{8,9},{9,10},{10,1... | collective-permute-start | bytes 6881288 | tf_op jit(solution)/gta,gtb->gab/dot_general | solution.py:19
  462.7 99.3 %collective-permute-start.1 = (bf16[1,1,160,7168]{3,2,1,0:T(8,128)(2,1)S(1)}, bf16[1,1,160,7168]{3,2,1,0:T(8,128)(2,1)}, u32[]{:S(2)}, u32[]{:S(2)}) collective-permute-start(bf16[1,1,160,7168]{3,2,1,0:T(8,128)(2,1)S(1)} %collective-permute-done), channel_id=8, source_target_pairs={{0,15},{1,0},{2,1},{3,2},{4,3},{5,4},{6,5},{7,6},{8,7},{9,8},{10,9... | collective-permute-start | bytes 6881288 | tf_op jit(solution)/gta,gtb->gab/dot_general | solution.py:19
  467.3 94.7 %collective-permute-start.3 = (bf16[1,1,160,7168]{3,2,1,0:T(8,128)(2,1)}, bf16[1,1,160,7168]{3,2,1,0:T(8,128)(2,1)}, u32[]{:S(2)}, u32[]{:S(2)}) collective-permute-start(bf16[1,1,160,7168]{3,2,1,0:T(8,128)(2,1)} %collective-permute-done.2), channel_id=9, source_target_pairs={{0,1},{1,2},{2,3},{3,4},{4,5},{5,6},{6,7},{7,8},{8,9},{9,10},{10,1... | collective-permute-start | bytes 6881288 | tf_op jit(solution)/gta,gtb->gab/dot_general | solution.py:19
  562.0 98.6 %collective-permute-start = (bf16[1,1,160,7168]{3,2,1,0:T(8,128)(2,1)}, bf16[1,1,160,7168]{3,2,1,0:T(8,128)(2,1)S(1)}, u32[]{:S(2)}, u32[]{:S(2)}) collective-permute-start(bf16[1,1,160,7168]{3,2,1,0:T(8,128)(2,1)} %get-tuple-element.146), channel_id=6, source_target_pairs={{0,15},{1,0},{2,1},{3,2},{4,3},{5,4},{6,5},{7,6},{8,7},{9,8},{10,9... | collective-permute-start | bytes 6881288 | tf_op jit(solution)/gta,gtb->gab/dot_general | solution.py:19
  566.6 130.3 %collective-permute-start.2 = (bf16[1,1,160,7168]{3,2,1,0:T(8,128)(2,1)}, bf16[1,1,160,7168]{3,2,1,0:T(8,128)(2,1)}, u32[]{:S(2)}, u32[]{:S(2)}) collective-permute-start(bf16[1,1,160,7168]{3,2,1,0:T(8,128)(2,1)} %get-tuple-element.148), channel_id=7, source_target_pairs={{0,1},{1,2},{2,3},{3,4},{4,5},{5,6},{6,7},{7,8},{8,9},{9,10},{10,1... | collective-permute-start | bytes 6881288 | tf_op jit(solution)/gta,gtb->gab/dot_general | solution.py:19
  660.5 93.8 %collective-permute-start.1 = (bf16[1,1,160,7168]{3,2,1,0:T(8,128)(2,1)S(1)}, bf16[1,1,160,7168]{3,2,1,0:T(8,128)(2,1)}, u32[]{:S(2)}, u32[]{:S(2)}) collective-permute-start(bf16[1,1,160,7168]{3,2,1,0:T(8,128)(2,1)S(1)} %collective-permute-done), channel_id=8, source_target_pairs={{0,15},{1,0},{2,1},{3,2},{4,3},{5,4},{6,5},{7,6},{8,7},{9,8},{10,9... | collective-permute-start | bytes 6881288 | tf_op jit(solution)/gta,gtb->gab/dot_general | solution.py:19
  696.9 67.1 %collective-permute-start.3 = (bf16[1,1,160,7168]{3,2,1,0:T(8,128)(2,1)}, bf16[1,1,160,7168]{3,2,1,0:T(8,128)(2,1)}, u32[]{:S(2)}, u32[]{:S(2)}) collective-permute-start(bf16[1,1,160,7168]{3,2,1,0:T(8,128)(2,1)} %collective-permute-done.2), channel_id=9, source_target_pairs={{0,1},{1,2},{2,3},{3,4},{4,5},{5,6},{6,7},{7,8},{8,9},{9,10},{10,1... | collective-permute-start | bytes 6881288 | tf_op jit(solution)/gta,gtb->gab/dot_general | solution.py:19
  764.0 68.1 %collective-permute-start.2 = (bf16[1,1,160,7168]{3,2,1,0:T(8,128)(2,1)}, bf16[1,1,160,7168]{3,2,1,0:T(8,128)(2,1)}, u32[]{:S(2)}, u32[]{:S(2)}) collective-permute-start(bf16[1,1,160,7168]{3,2,1,0:T(8,128)(2,1)} %get-tuple-element.148), channel_id=7, source_target_pairs={{0,1},{1,2},{2,3},{3,4},{4,5},{5,6},{6,7},{7,8},{8,9},{9,10},{10,1... | collective-permute-start | bytes 6881288 | tf_op jit(solution)/gta,gtb->gab/dot_general | solution.py:19
  814.1 81.2 %collective-permute-start.1 = (bf16[1,1,160,7168]{3,2,1,0:T(8,128)(2,1)S(1)}, bf16[1,1,160,7168]{3,2,1,0:T(8,128)(2,1)}, u32[]{:S(2)}, u32[]{:S(2)}) collective-permute-start(bf16[1,1,160,7168]{3,2,1,0:T(8,128)(2,1)S(1)} %collective-permute-done), channel_id=8, source_target_pairs={{0,15},{1,0},{2,1},{3,2},{4,3},{5,4},{6,5},{7,6},{8,7},{9,8},{10,9... | collective-permute-start | bytes 6881288 | tf_op jit(solution)/gta,gtb->gab/dot_general | solution.py:19
  832.2 96.4 %collective-permute-start.3 = (bf16[1,1,160,7168]{3,2,1,0:T(8,128)(2,1)}, bf16[1,1,160,7168]{3,2,1,0:T(8,128)(2,1)}, u32[]{:S(2)}, u32[]{:S(2)}) collective-permute-start(bf16[1,1,160,7168]{3,2,1,0:T(8,128)(2,1)} %collective-permute-done.2), channel_id=9, source_target_pairs={{0,1},{1,2},{2,3},{3,4},{4,5},{5,6},{6,7},{7,8},{8,9},{9,10},{10,1... | collective-permute-start | bytes 6881288 | tf_op jit(solution)/gta,gtb->gab/dot_general | solution.py:19
  928.6 60.4 %collective-permute-start = (bf16[1,1,160,7168]{3,2,1,0:T(8,128)(2,1)}, bf16[1,1,160,7168]{3,2,1,0:T(8,128)(2,1)S(1)}, u32[]{:S(2)}, u32[]{:S(2)}) collective-permute-start(bf16[1,1,160,7168]{3,2,1,0:T(8,128)(2,1)} %get-tuple-element.146), channel_id=6, source_target_pairs={{0,15},{1,0},{2,1},{3,2},{4,3},{5,4},{6,5},{7,6},{8,7},{9,8},{10,9... | collective-permute-start | bytes 6881288 | tf_op jit(solution)/gta,gtb->gab/dot_general | solution.py:19
  928.6 80.5 %collective-permute-start.2 = (bf16[1,1,160,7168]{3,2,1,0:T(8,128)(2,1)}, bf16[1,1,160,7168]{3,2,1,0:T(8,128)(2,1)}, u32[]{:S(2)}, u32[]{:S(2)}) collective-permute-start(bf16[1,1,160,7168]{3,2,1,0:T(8,128)(2,1)} %get-tuple-element.148), channel_id=7, source_target_pairs={{0,1},{1,2},{2,3},{3,4},{4,5},{5,6},{6,7},{7,8},{8,9},{9,10},{10,1... | collective-permute-start | bytes 6881288 | tf_op jit(solution)/gta,gtb->gab/dot_general | solution.py:19
  989.0 72.7 %collective-permute-start.1 = (bf16[1,1,160,7168]{3,2,1,0:T(8,128)(2,1)S(1)}, bf16[1,1,160,7168]{3,2,1,0:T(8,128)(2,1)}, u32[]{:S(2)}, u32[]{:S(2)}) collective-permute-start(bf16[1,1,160,7168]{3,2,1,0:T(8,128)(2,1)S(1)} %collective-permute-done), channel_id=8, source_target_pairs={{0,15},{1,0},{2,1},{3,2},{4,3},{5,4},{6,5},{7,6},{8,7},{9,8},{10,9... | collective-permute-start | bytes 6881288 | tf_op jit(solution)/gta,gtb->gab/dot_general | solution.py:19
  1009.1 52.6 %collective-permute-start.3 = (bf16[1,1,160,7168]{3,2,1,0:T(8,128)(2,1)}, bf16[1,1,160,7168]{3,2,1,0:T(8,128)(2,1)}, u32[]{:S(2)}, u32[]{:S(2)}) collective-permute-start(bf16[1,1,160,7168]{3,2,1,0:T(8,128)(2,1)} %collective-permute-done.2), channel_id=9, source_target_pairs={{0,1},{1,2},{2,3},{3,4},{4,5},{5,6},{6,7},{7,8},{8,9},{9,10},{10,1... | collective-permute-start | bytes 6881288 | tf_op jit(solution)/gta,gtb->gab/dot_general | solution.py:19
  1102.3 50.1 %collective-permute-start.4 = (bf16[1,1,160,7168]{3,2,1,0:T(8,128)(2,1)}, bf16[1,1,160,7168]{3,2,1,0:T(8,128)(2,1)S(1)}, u32[]{:S(2)}, u32[]{:S(2)}) collective-permute-start(bf16[1,1,160,7168]{3,2,1,0:T(8,128)(2,1)} %get-tuple-element.179), channel_id=12, source_target_pairs={{0,15},{1,0},{2,1},{3,2},{4,3},{5,4},{6,5},{7,6},{8,7},{9,8},{10,9... | collective-permute-start | bytes 6881288 | tf_op jit(solution)/gta,gtb->gab/dot_general | solution.py:19
  1106.8 51.5 %collective-permute-start.6 = (bf16[1,1,160,7168]{3,2,1,0:T(8,128)(2,1)}, bf16[1,1,160,7168]{3,2,1,0:T(8,128)(2,1)}, u32[]{:S(2)}, u32[]{:S(2)}) collective-permute-start(bf16[1,1,160,7168]{3,2,1,0:T(8,128)(2,1)} %get-tuple-element.181), channel_id=13, source_target_pairs={{0,1},{1,2},{2,3},{3,4},{4,5},{5,6},{6,7},{7,8},{8,9},{9,10},{10,1... | collective-permute-start | bytes 6881288 | tf_op jit(solution)/gta,gtb->gab/dot_general | solution.py:19
  1152.4 50.1 %collective-permute-start.5 = (bf16[1,1,160,7168]{3,2,1,0:T(8,128)(2,1)S(1)}, bf16[1,1,160,7168]{3,2,1,0:T(8,128)(2,1)S(1)}, u32[]{:S(2)}, u32[]{:S(2)}) collective-permute-start(bf16[1,1,160,7168]{3,2,1,0:T(8,128)(2,1)S(1)} %collective-permute-done.4), channel_id=14, source_target_pairs={{0,15},{1,0},{2,1},{3,2},{4,3},{5,4},{6,5},{7,6},{8,7},{9,8},{10,9... | collective-permute-start | bytes 6881288 | tf_op jit(solution)/gta,gtb->gab/dot_general | solution.py:19
  1208.5 51.6 %collective-permute-start.6 = (bf16[1,1,160,7168]{3,2,1,0:T(8,128)(2,1)}, bf16[1,1,160,7168]{3,2,1,0:T(8,128)(2,1)}, u32[]{:S(2)}, u32[]{:S(2)}) collective-permute-start(bf16[1,1,160,7168]{3,2,1,0:T(8,128)(2,1)} %get-tuple-element.181), channel_id=13, source_target_pairs={{0,1},{1,2},{2,3},{3,4},{4,5},{5,6},{6,7},{7,8},{8,9},{9,10},{10,1... | collective-permute-start | bytes 6881288 | tf_op jit(solution)/gta,gtb->gab/dot_general | solution.py:19
  1255.5 57.1 %collective-permute-start.5 = (bf16[1,1,160,7168]{3,2,1,0:T(8,128)(2,1)S(1)}, bf16[1,1,160,7168]{3,2,1,0:T(8,128)(2,1)S(1)}, u32[]{:S(2)}, u32[]{:S(2)}) collective-permute-start(bf16[1,1,160,7168]{3,2,1,0:T(8,128)(2,1)S(1)} %collective-permute-done.4), channel_id=14, source_target_pairs={{0,15},{1,0},{2,1},{3,2},{4,3},{5,4},{6,5},{7,6},{8,7},{9,8},{10,9... | collective-permute-start | bytes 6881288 | tf_op jit(solution)/gta,gtb->gab/dot_general | solution.py:19
  1260.2 52.5 %collective-permute-start.7 = (bf16[1,1,160,7168]{3,2,1,0:T(8,128)(2,1)}, bf16[1,1,160,7168]{3,2,1,0:T(8,128)(2,1)}, u32[]{:S(2)}, u32[]{:S(2)}) collective-permute-start(bf16[1,1,160,7168]{3,2,1,0:T(8,128)(2,1)} %collective-permute-done.6), channel_id=15, source_target_pairs={{0,1},{1,2},{2,3},{3,4},{4,5},{5,6},{6,7},{7,8},{8,9},{9,10},{10,1... | collective-permute-start | bytes 6881288 | tf_op jit(solution)/gta,gtb->gab/dot_general | solution.py:19
  1318.5 51.5 %collective-permute-start.6 = (bf16[1,1,160,7168]{3,2,1,0:T(8,128)(2,1)}, bf16[1,1,160,7168]{3,2,1,0:T(8,128)(2,1)}, u32[]{:S(2)}, u32[]{:S(2)}) collective-permute-start(bf16[1,1,160,7168]{3,2,1,0:T(8,128)(2,1)} %get-tuple-element.181), channel_id=13, source_target_pairs={{0,1},{1,2},{2,3},{3,4},{4,5},{5,6},{6,7},{7,8},{8,9},{9,10},{10,1... | collective-permute-start | bytes 6881288 | tf_op jit(solution)/gta,gtb->gab/dot_general | solution.py:19
  1364.2 58.3 %collective-permute-start.5 = (bf16[1,1,160,7168]{3,2,1,0:T(8,128)(2,1)S(1)}, bf16[1,1,160,7168]{3,2,1,0:T(8,128)(2,1)S(1)}, u32[]{:S(2)}, u32[]{:S(2)}) collective-permute-start(bf16[1,1,160,7168]{3,2,1,0:T(8,128)(2,1)S(1)} %collective-permute-done.4), channel_id=14, source_target_pairs={{0,15},{1,0},{2,1},{3,2},{4,3},{5,4},{6,5},{7,6},{8,7},{9,8},{10,9... | collective-permute-start | bytes 6881288 | tf_op jit(solution)/gta,gtb->gab/dot_general | solution.py:19
  1370.0 52.5 %collective-permute-start.7 = (bf16[1,1,160,7168]{3,2,1,0:T(8,128)(2,1)}, bf16[1,1,160,7168]{3,2,1,0:T(8,128)(2,1)}, u32[]{:S(2)}, u32[]{:S(2)}) collective-permute-start(bf16[1,1,160,7168]{3,2,1,0:T(8,128)(2,1)} %collective-permute-done.6), channel_id=15, source_target_pairs={{0,1},{1,2},{2,3},{3,4},{4,5},{5,6},{6,7},{7,8},{8,9},{9,10},{10,1... | collective-permute-start | bytes 6881288 | tf_op jit(solution)/gta,gtb->gab/dot_general | solution.py:19
  1423.9 50.1 %collective-permute-start.4 = (bf16[1,1,160,7168]{3,2,1,0:T(8,128)(2,1)}, bf16[1,1,160,7168]{3,2,1,0:T(8,128)(2,1)S(1)}, u32[]{:S(2)}, u32[]{:S(2)}) collective-permute-start(bf16[1,1,160,7168]{3,2,1,0:T(8,128)(2,1)} %get-tuple-element.179), channel_id=12, source_target_pairs={{0,15},{1,0},{2,1},{3,2},{4,3},{5,4},{6,5},{7,6},{8,7},{9,8},{10,9... | collective-permute-start | bytes 6881288 | tf_op jit(solution)/gta,gtb->gab/dot_general | solution.py:19
  1428.4 51.5 %collective-permute-start.6 = (bf16[1,1,160,7168]{3,2,1,0:T(8,128)(2,1)}, bf16[1,1,160,7168]{3,2,1,0:T(8,128)(2,1)}, u32[]{:S(2)}, u32[]{:S(2)}) collective-permute-start(bf16[1,1,160,7168]{3,2,1,0:T(8,128)(2,1)} %get-tuple-element.181), channel_id=13, source_target_pairs={{0,1},{1,2},{2,3},{3,4},{4,5},{5,6},{6,7},{7,8},{8,9},{9,10},{10,1... | collective-permute-start | bytes 6881288 | tf_op jit(solution)/gta,gtb->gab/dot_general | solution.py:19
  1474.0 58.3 %collective-permute-start.5 = (bf16[1,1,160,7168]{3,2,1,0:T(8,128)(2,1)S(1)}, bf16[1,1,160,7168]{3,2,1,0:T(8,128)(2,1)S(1)}, u32[]{:S(2)}, u32[]{:S(2)}) collective-permute-start(bf16[1,1,160,7168]{3,2,1,0:T(8,128)(2,1)S(1)} %collective-permute-done.4), channel_id=14, source_target_pairs={{0,15},{1,0},{2,1},{3,2},{4,3},{5,4},{6,5},{7,6},{8,7},{9,8},{10,9... | collective-permute-start | bytes 6881288 | tf_op jit(solution)/gta,gtb->gab/dot_general | solution.py:19
  1479.8 52.5 %collective-permute-start.7 = (bf16[1,1,160,7168]{3,2,1,0:T(8,128)(2,1)}, bf16[1,1,160,7168]{3,2,1,0:T(8,128)(2,1)}, u32[]{:S(2)}, u32[]{:S(2)}) collective-permute-start(bf16[1,1,160,7168]{3,2,1,0:T(8,128)(2,1)} %collective-permute-done.6), channel_id=15, source_target_pairs={{0,1},{1,2},{2,3},{3,4},{4,5},{5,6},{6,7},{7,8},{8,9},{9,10},{10,1... | collective-permute-start | bytes 6881288 | tf_op jit(solution)/gta,gtb->gab/dot_general | solution.py:19
  (9 other events, 205.3 us)
Sparse Core Ops, SparseCore 0:
  13.8 229.9 all-gather.4
  410.4 546.8 reduce-scatter.3
where the time goes:
time: 1580 us; the launch traced here: 1570 us
  matrix products  767 us (49%)
  waiting for transfers between devices  608 us (38%)
  starting transfers between devices  80 us (5%)
  local copies, waits for them, and re-layouts  56.5 us (4%)
  other arithmetic  25.8 us (2%)
    dot_general x16, matrix products, by_group(): jnp.einsum('gta,gtb->gab', a, b, preferred_element_type=jnp.float32)  601 us
    dot_general x34, waiting for transfers between devices, by_group(): jnp.einsum('gta,gtb->gab', a, b, preferred_element_type=jnp.float32)  381 us
    unnamed x4, waiting for transfers between devices  227 us
    dot_general x1, matrix products, step(): d_hidden = jnp.dot(dy, w_down.T, preferred_element_type=jnp.float32)  90.9 us
    dot_general x34, starting transfers between devices, by_group(): jnp.einsum('gta,gtb->gab', a, b, preferred_element_type=jnp.float32)  79.9 us
    dot_general x1, matrix products, step(): dx = jnp.dot(d_pre, w_in.T)  75.5 us
    dot_general x9, local copies, waits for them, and re-layouts, by_group(): jnp.einsum('gta,gtb->gab', a, b, preferred_element_type=jnp.float32)  45.2 us
  transfers between devices with their start and end apart: 36, of which 22 were waited for; matrix products, arithmetic and copies ran while one was open for 53% of the time, Pallas kernels for 0%

commit v1 on v0

v1 whole, which is shorter than its diff:
```python
import functools

import jax
import jax.numpy as jnp
from jax import lax
from jax.experimental import pallas as pl
from jax.experimental.pallas import tpu as pltpu

MESH = pl.DeviceIdType.MESH
BF16, F32 = jnp.bfloat16, jnp.float32
NY, NZ, NC = 2, 4, 2
RING = 3
OWN = 5
WINDOW = 2
LAST = 5
ROOT = 0.7978845608028654
CUBE = 0.044715


def bwd_kernel(
    dims,
    x_ref, dy_ref, pre_ref, win_ref, wdn_ref,
    dx_ref, dwin_ref, dwdn_ref, fx_ref, fdy_ref,
    dpre, hidt, in_r, in_l, in_d, in_y,
    rz, ry, rd, szp, szm, sy, sd, rx, sx, lsem,
    r_r, r_l, r_d, r_y, s_r, s_l, s_d, s_y,
    rxz, sxz, rxy, sxy, rxd, sxd, cred,
):
    rows, d, ff, tn, nch, fn = dims
    nt = d // tn
    ck = d // nch
    total = NY * NZ * NC * rows
    t = lax.axis_index("tp")
    c = t % NC
    z = (t // NC) % NZ
    y = t // (NC * NZ)
    yz = y * NZ + z
    p_zp, p_zm = t + NC, t - NC
    p_y = ((1 - y) * NZ + z) * NC + c
    p_d = yz * NC + (1 - c)
    first, last = z == 0, z == NZ - 1

    def remote(src, dst, ssem, rsem, to):
        return pltpu.make_async_remote_copy(
            src, dst, ssem, rsem, device_id={"tp": to}, device_id_type=MESH
        )

    def signal(sem, to):
        pl.semaphore_signal(sem, inc=1, device_id={"tp": to}, device_id_type=MESH)

    def cols(j, width):
        return pl.ds(pl.multiple_of(j * width, width), width)

    def loop(n, body):
        def step(i, carry):
            body(i)
            return carry

        lax.fori_loop(0, n, step, 0)

    barrier = pltpu.get_barrier_semaphore()
    signal(barrier, p_y)
    signal(barrier, p_d)

    @pl.when(jnp.logical_not(last))
    def _():
        signal(barrier, p_zp)

    @pl.when(jnp.logical_not(first))
    def _():
        signal(barrier, p_zm)

    pl.semaphore_wait(barrier, 4 - jnp.where(first | last, 1, 0))

    def zcopy_p(zb, q, src=None):
        ref = fdy_ref.at[y * NZ + zb, c, :, cols(q, ck)]
        return remote(ref if src is None else src, ref, szp.at[zb, q], rz.at[zb, q], p_zp)

    def zcopy_m(zb, q, src=None):
        ref = fdy_ref.at[y * NZ + zb, c, :, cols(q, ck)]
        return remote(ref if src is None else src, ref, szm.at[zb, q], rz.at[zb, q], p_zm)

    def ycopy(zb, q, src=None):
        ref = fdy_ref.at[y * NZ + zb, c, :, cols(q, ck)]
        return remote(ref if src is None else src, ref, sy.at[zb, q], ry.at[zb, q], p_y)

    def dcopy(b, q, src=None):
        ref = fdy_ref.at[b, c, :, cols(q, ck)]
        return remote(ref if src is None else src, ref, sd.at[b, q], rd.at[b, q], p_d)

    def xcopy(k, to):
        return remote(x_ref, fx_ref.at[yz, c], sx.at[k], rx.at[k], to)

    def phase1(wdn, dyu, preu):
        w_load = pltpu.make_async_copy(wdn_ref, wdn, lsem.at[0])
        own_dy = pltpu.make_async_copy(dy_ref, dyu.at[c], lsem.at[1])
        own_x = pltpu.make_async_copy(x_ref, dyu.at[1 - c], lsem.at[2])
        own_dy.start()
        own_x.start()

        def send_own(q):
            src = dy_ref.at[:, cols(q, ck)]

            @pl.when(jnp.logical_not(last))
            def _():
                zcopy_p(z, q, src).start()

            @pl.when(jnp.logical_not(first))
            def _():
                zcopy_m(z, q, src).start()

            ycopy(z, q, src).start()
            dcopy(yz, q, src).start()

        loop(nch, send_own)

        @pl.when(first)
        def _():
            xcopy(0, p_zp).start()

        @pl.when(last)
        def _():
            xcopy(1, p_zm).start()

        own_dy.wait()
        own_x.wait()
        put_dy = pltpu.make_async_copy(dyu.at[c], fdy_ref.at[yz, c], lsem.at[1])
        put_x = pltpu.make_async_copy(dyu.at[1 - c], fx_ref.at[yz, c], lsem.at[2])
        put_dy.start()
        put_x.start()
        w_load.start()

        hr = preu.shape[1] // 128 * 128

        def hidden(r):
            get = pltpu.make_async_copy(
                pre_ref.at[pl.ds(pl.multiple_of(r * hr, hr), hr)], preu.at[0, pl.ds(0, hr)], lsem.at[3]
            )
            get.start()
            get.wait()

            def part(n):
                p = preu[0, pl.ds(0, hr), cols(n, 128)].astype(F32)
                th = jnp.tanh(ROOT * (p + CUBE * (p * p * p)))
                h = (p * (0.5 * (1.0 + th))).astype(BF16)
                hidt[cols(n, 128), cols(r, hr)] = h.T

            loop(ff // 128, part)

        loop(total // hr, hidden)
        put_dy.wait()
        put_x.wait()
        w_load.wait()

        def m1(u):
            get = pltpu.make_async_copy(fdy_ref.at[u], dyu, lsem.at[1])
            get_pre = pltpu.make_async_copy(
                pre_ref.at[pl.ds(pl.multiple_of(u * (NC * rows), NC * rows), NC * rows)], preu.at[0, pl.ds(0, NC * rows)], lsem.at[3]
            )
            get.start()
            get_pre.start()
            get.wait()
            get_pre.wait()

            def part(n):
                acc = lax.dot_general(
                    dyu[...].reshape(NC * rows, d), wdn[cols(n, fn), :], (((1,), (1,)), ((), ())),
                    preferred_element_type=F32,
                )
                p = preu[0, pl.ds(0, NC * rows), cols(n, fn)].astype(F32)
                pp = p * p
                th = jnp.tanh(ROOT * (p + CUBE * (p * pp)))
                slope = 0.5 * (1.0 + th) + (0.5 * p) * (1.0 - th * th) * (ROOT * (1.0 + 3.0 * CUBE * pp))
                dpre[u, :, :, cols(n, fn)] = (acc * slope).astype(BF16).reshape(NC, rows, fn)

            loop(ff // fn, part)

        def wait_d(b):
            loop(nch, lambda q: dcopy_in(b, q).wait_recv())

        def dcopy_in(b, q):
            ref = fdy_ref.at[b, 1 - c, :, cols(q, ck)]
            return remote(ref, ref, sd.at[b, q], rd.at[b, q], p_d)

        def ycopy_in(zb, q):
            ref = fdy_ref.at[(1 - y) * NZ + zb, c, :, cols(q, ck)]
            return remote(ref, ref, sy.at[zb, q], ry.at[zb, q], p_y)

        def pass_row(zb):
            def piece(q):
                zcopy_p(zb, q).wait_recv()

                @pl.when((zb < z) & (z < NZ - 1))
                def _():
                    zcopy_p(zb, q).start()

                @pl.when((zb > z) & (z > 0))
                def _():
                    zcopy_m(zb, q).start()

                ycopy(zb, q).start()
                dcopy(y * NZ + zb, q).start()

            loop(nch, piece)

        def pass_other(zb):
            def piece(q):
                ycopy_in(zb, q).wait_recv()
                dcopy((1 - y) * NZ + zb, q).start()

            loop(nch, piece)

        def unit(b):
            wait_d(b)
            m1(b)

        o1 = jnp.where(z == 0, 1, z - 1)
        o2 = jnp.where(z == NZ - 1, 1, jnp.where(z == 2, 3, 2))
        o3 = jnp.where(z < 2, 3, 0)
        inner = (z == 1) | (z == 2)
        other = (1 - y) * NZ

        unit(yz)
        pass_row(o1)

        @pl.when(z == 1)
        def _():
            xcopy(0, p_zp).start()

        @pl.when(inner)
        def _():
            pass_row(o2)

        @pl.when(z == 2)
        def _():
            xcopy(1, p_zm).start()

        unit(y * NZ + o1)
        pass_other(z)
        unit(other + z)

        @pl.when(jnp.logical_not(inner))
        def _():
            pass_row(o2)

        unit(y * NZ + o2)
        pass_other(o1)
        pass_row(o3)

        @pl.when(z == 2)
        def _():
            xcopy(0, p_zp).start()

        @pl.when(z == 1)
        def _():
            xcopy(1, p_zm).start()

        unit(other + o1)
        unit(y * NZ + o3)
        pass_other(o2)
        unit(other + o2)
        pass_other(o3)
        unit(other + o3)

        def sent(q):
            def row(zb):
                @pl.when((zb <= z) & (z < NZ - 1))
                def _():
                    zcopy_p(zb, q).wait_send()

                @pl.when((zb >= z) & (z > 0))
                def _():
                    zcopy_m(zb, q).wait_send()

                ycopy(zb, q).wait_send()

            loop(NZ, row)
            loop(NY * NZ, lambda b: dcopy(b, q).wait_send())

        loop(nch, sent)

        @pl.when(jnp.logical_not(last))
        def _():
            xcopy(0, p_zp).wait_send()
            remote(x_ref, fx_ref.at[yz + 1, c], sx.at[1], rx.at[1], p_zm).wait_recv()

        @pl.when(jnp.logical_not(first))
        def _():
            xcopy(1, p_zm).wait_send()
            remote(x_ref, fx_ref.at[yz - 1, c], sx.at[0], rx.at[0], p_zp).wait_recv()

    pl.run_scoped(
        phase1,
        pltpu.VMEM((ff, d), BF16),
        pltpu.VMEM((NC, rows, d), BF16),
        pltpu.VMEM((1, max(NC * rows, 128), ff), BF16),
    )

    def phase2(own, out_r, out_l, out_d, out_y, wt, dyt, xt, xtt, odn, oin, odx, ls):
        far = jnp.maximum(z, NZ - 1 - z)
        steps = nt + LAST

        def inside(j):
            return (j >= 0) & (j < nt)

        def rcopy(slot, k):
            return remote(out_r.at[slot, k], in_r.at[slot, k], s_r.at[slot, k], r_r.at[slot, k], p_zp)

        def lcopy(slot, k):
            return remote(out_l.at[slot, k], in_l.at[slot, k], s_l.at[slot, k], r_l.at[slot, k], p_zm)

        def dsum(slot):
            return remote(out_d.at[slot], in_d.at[slot], s_d.at[slot], r_d.at[slot], p_d)

        def ysum(slot):
            return remote(out_y.at[slot], in_y.at[slot], s_y.at[slot], r_y.at[slot], p_y)

        def add_core(s):
            j = s - 1

            @pl.when(inside(j))
            def _():
                slot, ring = j % RING, j % OWN
                dsum(slot).wait_recv()

                def piece(b):
                    own[ring, b // NZ, b % NZ] += in_d[slot, b].astype(F32)

                loop(NY * NZ, piece)

        def along(s, away, edge, copy, inb, outb):
            behind = z if away == 1 else NZ - 1 - z
            j = s - 1 - behind

            @pl.when(inside(j))
            def _():
                slot, ring = j % RING, j % OWN
                for k in range(1, NZ):
                    zz = z + away * k

                    @pl.when((zz >= 0) & (zz < NZ))
                    def _():
                        @pl.when(j >= RING)
                        def _():
                            copy(slot, k - 1).wait_send()

                        @pl.when(edge)
                        def _():
                            def piece(h):
                                outb[slot, k - 1, h] = own[ring, h, zz].astype(BF16)

                            loop(NY, piece)

                        if k < NZ - 1:

                            @pl.when(jnp.logical_not(edge))
                            def _():
                                copy(slot, k).wait_recv()

                                def piece(h):
                                    outb[slot, k - 1, h] = (own[ring, h, zz] + inb[slot, k, h].astype(F32)).astype(BF16)

                                loop(NY, piece)

                        copy(slot, k - 1).start()

                @pl.when(jnp.logical_not(edge))
                def _():
                    copy(slot, 0).wait_recv()

                    def piece(h):
                        own[ring, h, z] += inb[slot, 0, h].astype(F32)

                    loop(NY, piece)

        def across(s):
            j = s - 1 - far

            @pl.when(inside(j))
            def _():
                slot, ring = j % RING, j % OWN

                @pl.when(j >= RING)
                def _():
                    ysum(slot).wait_send()

                out_y[slot] = own[ring, 1 - y, z].astype(BF16)
                ysum(slot).start()

        def put_dx(j):
            return pltpu.make_async_copy(odx.at[j % 2], dx_ref.at[:, cols(j, tn)], ls.at[5, j % 2])

        def finish(s):
            j = s - 2 - far

            @pl.when(inside(j))
            def _():
                slot, ring = j % RING, j % OWN

                @pl.when(j >= 2)
                def _():
                    put_dx(j - 2).wait()

                ysum(slot).wait_recv()
                odx[j % 2] = (own[ring, y, z] + in_y[slot].astype(F32)).astype(BF16)
                put_dx(j).start()

        def xz(j, away, stage, zb):
            ref = fx_ref.at[y * NZ + zb, c, :, cols(j, tn)]
            k = 0 if away == 1 else 1
            return remote(ref, ref, sxz.at[k, stage, j % RING], rxz.at[k, stage, j % RING], p_zp if away == 1 else p_zm)

        def xy(j, row):
            ref = fx_ref.at[pl.ds(row * NZ, NZ), c, :, cols(j, tn)]
            return remote(ref, ref, sxy.at[j % RING], rxy.at[j % RING], p_y)

        def xd(j, core):
            ref = fx_ref.at[:, core, :, cols(j, tn)]
            return remote(ref, ref, sxd.at[j % RING], rxd.at[j % RING], p_d)

        def send(j, make):
            @pl.when(j >= RING)
            def _():
                make(j - RING).wait_send()

            make(j).start()

        def get_x(j):
            return pltpu.make_async_copy(fx_ref.at[:, :, :, cols(j, tn)], xt.at[j % 2], ls.at[2, j % 2])

        inner = (z == 1) | (z == 2)

        def move_x(s):
            @pl.when(inside(s) & inner)
            def _():
                send(s, lambda j: xz(j, 1, 0, z - 1))
                send(s, lambda j: xz(j, -1, 0, z + 1))

            @pl.when(inside(s - 1))
            def _():
                @pl.when(z >= 2)
                def _():
                    xz(s - 1, 1, 0, z - 2).wait_recv()

                @pl.when(z < 2)
                def _():
                    xz(s - 1, -1, 0, z + 2).wait_recv()

                @pl.when(z == 2)
                def _():
                    send(s - 1, lambda j: xz(j, 1, 1, 0))

                @pl.when(z == 1)
                def _():
                    send(s - 1, lambda j: xz(j, -1, 1, 3))

            @pl.when(inside(s - 2))
            def _():
                @pl.when(z == NZ - 1)
                def _():
                    xz(s - 2, 1, 1, 0).wait_recv()

                @pl.when(z == 0)
                def _():
                    xz(s - 2, -1, 1, NZ - 1).wait_recv()

                send(s - 2, lambda j: xy(j, y))

            @pl.when(inside(s - 3))
            def _():
                xy(s - 3, 1 - y).wait_recv()
                send(s - 3, lambda j: xd(j, c))

            @pl.when(inside(s - 4))
            def _():
                xd(s - 4, 1 - c).wait_recv()
                get_x(s - 4).start()

        def get_w(j):
            return pltpu.make_async_copy(win_ref.at[cols(j, tn)], wt.at[j % 2], ls.at[0, j % 2])

        def get_dy(j):
            return pltpu.make_async_copy(fdy_ref.at[:, :, :, cols(j, tn)], dyt.at[j % 2], ls.at[1, j % 2])

        def put_dn(j):
            return pltpu.make_async_copy(odn.at[j % 2], dwdn_ref.at[:, cols(j, tn)], ls.at[3, j % 2])

        def put_in(j):
            return pltpu.make_async_copy(oin.at[j % 2], dwin_ref.at[cols(j, tn)], ls.at[4, j % 2])

        def term(j):
            slot, ring = j % RING, j % OWN
            get_w(j).wait()

            @pl.when(j + 1 < nt)
            def _():
                get_w(j + 1).start()

            @pl.when(j >= RING)
            def _():
                dsum(slot).wait_send()

            def dot(core, h):
                lhs = dpre[pl.ds(h * NZ, NZ), core].reshape(NZ * rows, ff)
                return lax.dot_general(
                    lhs, wt[j % 2], (((1,), (1,)), ((), ())), preferred_element_type=F32
                ).reshape(NZ, rows, tn)

            def theirs(h):
                out_d[slot, pl.ds(h * NZ, NZ)] = dot(1 - c, h).astype(BF16)

            loop(NY, theirs)
            dsum(slot).start()

            def ours(h):
                own[ring, h] = dot(c, h)

            loop(NY, ours)

        mh = ff // 4 if (ff // 4) % 16 == 0 else ff

        def down(j):
            get_dy(j).wait()

            @pl.when(j + 1 < nt)
            def _():
                get_dy(j + 1).start()

            @pl.when(j >= 2)
            def _():
                put_dn(j - 2).wait()

            def part(m):
                at = pl.ds(pl.multiple_of(m * mh, mh), mh)
                odn[j % 2, at] = jnp.dot(
                    hidt[at, :], dyt[j % 2].reshape(total, tn), preferred_element_type=F32
                ).astype(BF16)

            loop(ff // mh, part)
            put_dn(j).start()

        def inward(j):
            get_x(j).wait()

            @pl.when(j >= 2)
            def _():
                put_in(j - 2).wait()

            xtt[...] = xt[j % 2].reshape(total, tn).T

            def part(n):
                rhs = dpre[:, :, :, cols(n, fn)].reshape(total, fn)
                oin[j % 2, :, cols(n, fn)] = jnp.dot(xtt[...], rhs, preferred_element_type=F32).astype(BF16)

            loop(ff // fn, part)
            put_in(j).start()

        get_w(0).start()
        get_dy(0).start()

        def step(s):
            @pl.when(s >= WINDOW)
            def _():
                pl.semaphore_wait(cred.at[2], 1)
                pl.semaphore_wait(cred.at[3], 1)

                @pl.when(jnp.logical_not(last))
                def _():
                    pl.semaphore_wait(cred.at[0], 1)

                @pl.when(jnp.logical_not(first))
                def _():
                    pl.semaphore_wait(cred.at[1], 1)

            add_core(s)
            along(s, 1, first, rcopy, in_r, out_r)
            along(s, -1, last, lcopy, in_l, out_l)
            finish(s)
            across(s)
            move_x(s)

            @pl.when(s < steps - WINDOW)
            def _():
                signal(cred.at[2], p_y)
                signal(cred.at[3], p_d)

                @pl.when(jnp.logical_not(last))
                def _():
                    signal(cred.at[1], p_zp)

                @pl.when(jnp.logical_not(first))
                def _():
                    signal(cred.at[0], p_zm)

            @pl.when(s < nt)
            def _():
                term(s)
                down(s)

            @pl.when(inside(s - LAST))
            def _():
                inward(s - LAST)

        loop(steps, step)

        for j in range(nt - RING, nt):
            slot = j % RING
            for k in range(NZ - 1):

                @pl.when(z + k + 1 < NZ)
                def _():
                    rcopy(slot, k).wait_send()

                @pl.when(z - k - 1 >= 0)
                def _():
                    lcopy(slot, k).wait_send()

            dsum(slot).wait_send()
            ysum(slot).wait_send()
            xy(j, y).wait_send()
            xd(j, c).wait_send()

            @pl.when(inner)
            def _():
                xz(j, 1, 0, z - 1).wait_send()
                xz(j, -1, 0, z + 1).wait_send()

            @pl.when(z == 2)
            def _():
                xz(j, 1, 1, 0).wait_send()

            @pl.when(z == 1)
            def _():
                xz(j, -1, 1, 3).wait_send()

        for j in range(nt - 2, nt):
            put_dn(j).wait()
            put_in(j).wait()
            put_dx(j).wait()

    pl.run_scoped(
        phase2,
        pltpu.VMEM((OWN, NY, NZ, rows, tn), F32),
        pltpu.VMEM((RING, NZ - 1, NY, rows, tn), BF16),
        pltpu.VMEM((RING, NZ - 1, NY, rows, tn), BF16),
        pltpu.VMEM((RING, NY * NZ, rows, tn), BF16),
        pltpu.VMEM((RING, rows, tn), BF16),
        pltpu.VMEM((2, tn, ff), BF16),
        pltpu.VMEM((2, NY * NZ, NC, rows, tn), BF16),
        pltpu.VMEM((2, NY * NZ, NC, rows, tn), BF16),
        pltpu.VMEM((tn, total), BF16),
        pltpu.VMEM((2, ff, tn), BF16),
        pltpu.VMEM((2, tn, ff), BF16),
        pltpu.VMEM((2, rows, tn), BF16),
        pltpu.SemaphoreType.DMA((6, 2)),
    )


def call(rows, d, ff, tn, nch, fn, x, dy, pre, win, wdn):
    blocks = NY * NZ
    total = blocks * NC * rows
    dma = pltpu.SemaphoreType.DMA
    any_ = pl.BlockSpec(memory_space=pl.ANY)
    return pl.pallas_call(
        functools.partial(bwd_kernel, (rows, d, ff, tn, nch, fn)),
        name="bwd",
        out_shape=[
            jax.ShapeDtypeStruct((rows, d), BF16),
            jax.ShapeDtypeStruct((d, ff), BF16),
            jax.ShapeDtypeStruct((ff, d), BF16),
            jax.ShapeDtypeStruct((blocks, NC, rows, d), BF16),
            jax.ShapeDtypeStruct((blocks, NC, rows, d), BF16),
        ],
        in_specs=[any_] * 5,
        out_specs=[any_] * 5,
        scratch_shapes=[
            pltpu.VMEM((blocks, NC, rows, ff), BF16),
            pltpu.VMEM((ff, total), BF16),
            pltpu.VMEM((RING, NZ - 1, NY, rows, tn), BF16),
            pltpu.VMEM((RING, NZ - 1, NY, rows, tn), BF16),
            pltpu.VMEM((RING, blocks, rows, tn), BF16),
            pltpu.VMEM((RING, rows, tn), BF16),
            dma((NZ, nch)), dma((NZ, nch)), dma((blocks, nch)),
            dma((NZ, nch)), dma((NZ, nch)), dma((NZ, nch)), dma((blocks, nch)),
            dma((2,)), dma((2,)), dma((4,)),
            dma((RING, NZ - 1)), dma((RING, NZ - 1)), dma((RING,)), dma((RING,)),
            dma((RING, NZ - 1)), dma((RING, NZ - 1)), dma((RING,)), dma((RING,)),
            dma((2, 2, RING)), dma((2, 2, RING)), dma((RING,)), dma((RING,)), dma((RING,)), dma((RING,)),
            pltpu.SemaphoreType.REGULAR((4,)),
        ],
        compiler_params=pltpu.CompilerParams(
            collective_id=0, has_side_effects=True, vmem_limit_bytes=67043328
        ),
    )(x, dy, pre, win, wdn)


def solution(mesh):
    spec = jax.sharding.PartitionSpec
    rows_of, cols_of = spec(("dp", "tp"), None), spec("dp", "tp")

    def local(x, dy, pre, win, wdn):
        rows, d = x.shape
        ff = pre.shape[1]
        dx, dwin, dwdn, _, _ = call(rows, d, ff, 256, 4, 256, x, dy, pre, win, wdn)
        return dx, dwin, dwdn

    return jax.shard_map(
        local,
        mesh=mesh,
        in_specs=(rows_of, rows_of, cols_of, spec(None, "tp"), spec("tp", None)),
        out_specs=(rows_of, cols_of, rows_of),
        check_vma=False,
    )
```

time: 1580 us -> 596 us (0.38)
  matrix products: 767 us -> 0 us
  waiting for transfers between devices: 608 us -> 0 us
  Pallas kernels: 0 us -> 556 us
  starting transfers between devices: 80 us -> 0 us
  other arithmetic: 25.8 us -> 0.01 us
  local copies, waits for them, and re-layouts: 56.5 us -> 36.8 us
    dot_general x18 -> x0, matrix products: 767 us -> none  [the longest x16 601 us: by_group(): jnp.einsum('gta,gtb->gab', a, b, preferred_element_type=jnp.float32)]
    pallas_call x0 -> x1, Pallas kernels: none -> 556 us  [call(): pl.pallas_call(functools.partial(bwd_kernel, (rows, d, ff, tn, nch, fn)),...]
    dot_general x34 -> x0, waiting for transfers between devices: 381 us -> none  [by_group(): jnp.einsum('gta,gtb->gab', a, b, preferred_element_type=jnp.float32)]
    unnamed x4 -> x0, waiting for transfers between devices: 227 us -> none
    dot_general x34 -> x0, starting transfers between devices: 79.9 us -> none  [by_group(): jnp.einsum('gta,gtb->gab', a, b, preferred_element_type=jnp.float32)]
    dot_general x17 -> x0, local copies, waits for them, and re-layouts: 49.5 us -> none  [the longest x9 45.2 us: by_group(): jnp.einsum('gta,gtb->gab', a, b, preferred_element_type=jnp.float32)]
    unnamed x4 -> x17, local copies, waits for them, and re-layouts: 7.08 us -> 36.8 us
    reshape x1 -> x0, other arithmetic: 25.8 us -> none  [by_group(): return product.astype(jnp.bfloat16).reshape(-1, b.shape[-1])]
  transfers between devices with their start and end apart: 36 -> 0, of which waited for: 22 -> 0; matrix products, arithmetic and copies ran while one was open for 53% -> 0% of each run, Pallas kernels for 0% -> 0%
where the time goes in v1:
time: 596 us; the launch traced here: 593 us
  Pallas kernels  556 us (93%)
  local copies, waits for them, and re-layouts  36.8 us (6%)
    pallas_call x1, Pallas kernels, call(): pl.pallas_call(functools.partial(bwd_kernel, (rows, d, ff, tn, nch, fn)),...  556 us
    unnamed x17, local copies, waits for them, and re-layouts  36.8 us

profile of v1, /device:TPU:0, one launch (start us, length us, event | category | flops | bytes accessed | tf_op | source)
XLA Modules:
  0.0 593.2 jit_solution(15391246795567842093)
XLA Ops:
  0.6 555.7 %bwd.1 = (bf16[160,7168]{1,0:T(8,128)(2,1)}, bf16[7168,1792]{1,0:T(8,128)(2,1)}, bf16[1792,7168]{1,0:T(8,128)(2,1)}, bf16[8,2,160,7168]{3,2,1,0:T(8,128)(2,1)}, bf16[8,2,160,7168]{3,2,1,0:T(8,128)(2,1)}) custom-call(bf16[160,7168]{1,0:T(8,128)(2,1)} %x_ref.1, bf16[160,7168]{1,0:T(8,128)(2,1)} %dy_ref.1, bf16[2560,1792]{1,0:T(8,128)(2,1)} %pre_ref.1, ...), custom_call_target="tpu_custom_call" | custom-call | tf_op jit(solution)/shard_map/bwd/pallas_call | solution.py:664
  556.3 0.0 slice-start
  556.3 3.3 copy.11
  559.7 0.0 slice-start.1
  559.7 0.0 slice-start.2
  559.7 0.0 slice-start.3
  559.7 0.0 slice-start.4
  559.7 0.0 slice-start.5
  559.7 0.0 slice-start.6
  559.7 24.4 %copy.12 = bf16[7168,1792]{1,0:T(8,128)(2,1)} copy(bf16[7168,1792]{1,0:T(8,128)(2,1)} %get-tuple-element.13) | data formatting | bytes 51380224
  584.1 0.0 slice-done
  584.1 0.0 slice-done.1
  584.1 0.0 slice-done.2
  584.1 0.0 slice-done.3
  584.1 0.0 slice-done.4
  584.1 0.0 slice-done.5
  584.1 0.0 slice-done.6
  584.1 9.1 %copy.13 = bf16[1792,7168]{1,0:T(8,128)(2,1)} copy(bf16[1792,7168]{1,0:T(8,128)(2,1)S(1)} %bitcast.1) | data formatting | bytes 51380224
  (1 shorter events, 0.0 us)
Async XLA Ops:
  556.3 27.8 %slice-start = ((s8[25690112]{0:T(1024)(128)(4,1)}), s8[4194304]{0:T(1024)(128)(4,1)S(1)}, s32[]{:S(2)}) async-start(s8[25690112]{0:T(1024)(128)(4,1)} %bitcast), calls=%async_computation | async-start | bytes 8388608
  559.7 24.4 %slice-start.1 = ((s8[25690112]{0:T(1024)(128)(4,1)}), s8[4194304]{0:T(1024)(128)(4,1)S(1)}, s32[]{:S(2)}) async-start(s8[25690112]{0:T(1024)(128)(4,1)} %bitcast), calls=%async_computation.1 | async-start | bytes 8388608
  559.7 24.4 %slice-start.2 = ((s8[25690112]{0:T(1024)(128)(4,1)}), s8[4194304]{0:T(1024)(128)(4,1)S(1)}, s32[]{:S(2)}) async-start(s8[25690112]{0:T(1024)(128)(4,1)} %bitcast), calls=%async_computation.2 | async-start | bytes 8388608
  559.7 24.4 %slice-start.3 = ((s8[25690112]{0:T(1024)(128)(4,1)}), s8[4194304]{0:T(1024)(128)(4,1)S(1)}, s32[]{:S(2)}) async-start(s8[25690112]{0:T(1024)(128)(4,1)} %bitcast), calls=%async_computation.3 | async-start | bytes 8388608
  559.7 24.4 %slice-start.4 = ((s8[25690112]{0:T(1024)(128)(4,1)}), s8[4194304]{0:T(1024)(128)(4,1)S(1)}, s32[]{:S(2)}) async-start(s8[25690112]{0:T(1024)(128)(4,1)} %bitcast), calls=%async_computation.4 | async-start | bytes 8388608
  559.7 24.4 %slice-start.5 = ((s8[25690112]{0:T(1024)(128)(4,1)}), s8[4194304]{0:T(1024)(128)(4,1)S(1)}, s32[]{:S(2)}) async-start(s8[25690112]{0:T(1024)(128)(4,1)} %bitcast), calls=%async_computation.5 | async-start | bytes 8388608
  559.7 24.4 %slice-start.6 = ((s8[25690112]{0:T(1024)(128)(4,1)}), s8[524288]{0:T(1024)(128)(4,1)S(1)}, s32[]{:S(2)}) async-start(s8[25690112]{0:T(1024)(128)(4,1)} %bitcast), calls=%async_computation.6 | async-start | bytes 1048576

commit v2 on v1

v2 whole, which is shorter than its diff:
```python
import functools

import jax
import jax.numpy as jnp
from jax import lax
from jax.experimental import pallas as pl
from jax.experimental.pallas import tpu as pltpu

MESH = pl.DeviceIdType.MESH
BF16, F32 = jnp.bfloat16, jnp.float32
NY, NZ, NC = 2, 4, 2
RING = 4
OWN = 6
WINDOW = 2
TAIL = 4
LEAD = 5
ROOT = 0.7978845608028654
CUBE = 0.044715


def bwd_kernel(
    dims,
    x_ref, dy_ref, pre_ref, win_ref, wdn_ref,
    dx_ref, dwin_ref, dwdn_ref, fx_ref, fdy_ref,
    dpre, hidt, in_r, in_l, in_d, in_y, in_w, in_e,
    rz, ry, rd, szp, szm, sy, sd, rx, sx, lsem,
    r_r, r_l, r_d, r_y, r_w, r_e, s_r, s_l, s_d, s_y, s_w, s_e,
    rxz, sxz, rxy, sxy, rxd, sxd, cred,
):
    rows, d, ff, tn, nch, fn = dims
    nt = d // tn
    ck = d // nch
    total = NY * NZ * NC * rows
    t = lax.axis_index("tp")
    c = t % NC
    z = (t // NC) % NZ
    y = t // (NC * NZ)
    yz = y * NZ + z
    p_zp, p_zm = t + NC, t - NC
    p_y = ((1 - y) * NZ + z) * NC + c
    p_d = yz * NC + (1 - c)
    first, last = z == 0, z == NZ - 1

    def remote(src, dst, ssem, rsem, to):
        return pltpu.make_async_remote_copy(
            src, dst, ssem, rsem, device_id={"tp": to}, device_id_type=MESH
        )

    def signal(sem, to):
        pl.semaphore_signal(sem, inc=1, device_id={"tp": to}, device_id_type=MESH)

    def cols(j, width):
        return pl.ds(pl.multiple_of(j * width, width), width)

    def loop(n, body):
        def step(i, carry):
            body(i)
            return carry

        lax.fori_loop(0, n, step, 0)

    barrier = pltpu.get_barrier_semaphore()
    signal(barrier, p_y)
    signal(barrier, p_d)

    @pl.when(jnp.logical_not(last))
    def _():
        signal(barrier, p_zp)

    @pl.when(jnp.logical_not(first))
    def _():
        signal(barrier, p_zm)

    pl.semaphore_wait(barrier, 4 - jnp.where(first | last, 1, 0))

    inner = (z == 1) | (z == NZ - 2)
    edge = first | last

    def inside(j):
        return (j >= 0) & (j < nt)

    def xz(j, away, stage, zb, n=1):
        ref = fx_ref.at[pl.ds(y * NZ + zb, n), c, :, cols(j, tn)]
        k = 0 if away == 1 else 1
        return remote(ref, ref, sxz.at[k, stage, j % RING], rxz.at[k, stage, j % RING], p_zp if away == 1 else p_zm)

    def xy(j, row):
        ref = fx_ref.at[pl.ds(row * NZ, NZ), c, :, cols(j, tn)]
        return remote(ref, ref, sxy.at[j % RING], rxy.at[j % RING], p_y)

    def xd(j, core):
        ref = fx_ref.at[:, core, :, cols(j, tn)]
        return remote(ref, ref, sxd.at[j % RING], rxd.at[j % RING], p_d)

    def send(j, make):
        @pl.when(j >= RING)
        def _():
            make(j - RING).wait_send()

        make(j).start()

    def x_out(j, away, wait=False):
        end = 2 if away == 1 else 1

        def do(make):
            if wait:
                make(j).wait_send()
            else:
                send(j, make)

        @pl.when(z == end)
        def _():
            do(lambda i: xz(i, away, 0, 1, 2))

        @pl.when(z == NZ - 1 - end)
        def _():
            do(lambda i: xz(i, away, 0, 0 if away == 1 else NZ - 1))

    def move_x(s):
        @pl.when(inside(s))
        def _():
            x_out(s, 1)
            x_out(s, -1)

        @pl.when(inside(s - 2))
        def _():
            j = s - 2

            @pl.when(last)
            def _():
                xz(j, 1, 0, 1, 2).wait_recv()

            @pl.when(first)
            def _():
                xz(j, -1, 0, 1, 2).wait_recv()

            @pl.when(z == 2)
            def _():
                xz(j, 1, 0, 0).wait_recv()
                send(j, lambda i: xz(i, 1, 1, 0))

            @pl.when(z == 1)
            def _():
                xz(j, -1, 0, NZ - 1).wait_recv()
                send(j, lambda i: xz(i, -1, 1, NZ - 1))

        @pl.when(inside(s - 4))
        def _():
            j = s - 4

            @pl.when(last)
            def _():
                xz(j, 1, 1, 0).wait_recv()

            @pl.when(first)
            def _():
                xz(j, -1, 1, NZ - 1).wait_recv()

            send(j, lambda i: xy(i, y))

        @pl.when(inside(s - 6))
        def _():
            xy(s - 6, 1 - y).wait_recv()
            send(s - 6, lambda i: xd(i, c))

    def step_in():
        pl.semaphore_wait(cred.at[2], 1)
        pl.semaphore_wait(cred.at[3], 1)

        @pl.when(jnp.logical_not(last))
        def _():
            pl.semaphore_wait(cred.at[0], 1)

        @pl.when(jnp.logical_not(first))
        def _():
            pl.semaphore_wait(cred.at[1], 1)

    def step_out():
        signal(cred.at[2], p_y)
        signal(cred.at[3], p_d)

        @pl.when(jnp.logical_not(last))
        def _():
            signal(cred.at[1], p_zp)

        @pl.when(jnp.logical_not(first))
        def _():
            signal(cred.at[0], p_zm)

    def dy_at(b, core, q):
        return fdy_ref.at[b, core, :, cols(q, ck)]

    def zcopy(row, zb, q, away, src=None):
        ref = dy_at(row * NZ + zb, c, q)
        back = row != y
        rsem = rz.at[zb, jnp.where(back, nch, q)]
        if away == 1:
            return remote(ref if src is None else src, ref, szp.at[zb, jnp.where(back, nch, q)], rsem, p_zp)
        return remote(ref if src is None else src, ref, szm.at[zb, jnp.where(back, nch, q)], rsem, p_zm)

    def ycopy(row, zb, q, src=None):
        ref = dy_at(row * NZ + zb, c, q)
        return remote(ref if src is None else src, ref, sy.at[zb, q], ry.at[zb, q], p_y)

    def dcopy(b, core, q, src=None):
        ref = dy_at(b, core, q)
        return remote(ref if src is None else src, ref, sd.at[b, q], rd.at[b, q], p_d)

    def xcopy(k, to, b):
        return remote(x_ref, fx_ref.at[b, c], sx.at[k], rx.at[k], to)

    def phase1(wdn, dyu, preu):
        w_load = pltpu.make_async_copy(wdn_ref, wdn, lsem.at[0])
        own_dy = pltpu.make_async_copy(dy_ref, dyu.at[c], lsem.at[1])
        own_x = pltpu.make_async_copy(x_ref, dyu.at[1 - c], lsem.at[2])
        own_dy.start()
        own_x.start()

        def send_own(q):
            src = dy_ref.at[:, cols(q, ck)]

            @pl.when(jnp.logical_not(last))
            def _():
                zcopy(y, z, q, 1, src).start()

            @pl.when(jnp.logical_not(first))
            def _():
                zcopy(y, z, q, -1, src).start()

            ycopy(y, z, q, src).start()
            dcopy(yz, c, q, src).start()

        loop(nch, send_own)
        own_dy.wait()
        own_x.wait()
        put_dy = pltpu.make_async_copy(dyu.at[c], fdy_ref.at[yz, c], lsem.at[1])
        put_x = pltpu.make_async_copy(dyu.at[1 - c], fx_ref.at[yz, c], lsem.at[2])
        put_dy.start()
        put_x.start()
        w_load.start()

        def pass_z(row, zb, q):
            @pl.when((zb < z) & (z < NZ - 1))
            def _():
                zcopy(row, zb, q, 1).start()

            @pl.when((zb > z) & (z > 0))
            def _():
                zcopy(row, zb, q, -1).start()

        def pass_row(zb, q):
            zcopy(y, zb, q, 1).wait_recv()
            pass_z(y, zb, q)

            @pl.when(q > 0)
            def _():
                ycopy(y, zb, q).start()

            dcopy(y * NZ + zb, c, q).start()

        def pass_back(zb):
            zcopy(1 - y, zb, 0, 1).wait_recv()
            pass_z(1 - y, zb, 0)
            dcopy((1 - y) * NZ + zb, c, 0).start()

        def pass_other(zb):
            def piece(q):
                ycopy(1 - y, zb, q + 1).wait_recv()
                dcopy((1 - y) * NZ + zb, c, q + 1).start()

            loop(nch - 1, piece)

        ycopy(1 - y, z, 0).wait_recv()

        @pl.when(jnp.logical_not(last))
        def _():
            zcopy(1 - y, z, 0, 1).start()

        @pl.when(jnp.logical_not(first))
        def _():
            zcopy(1 - y, z, 0, -1).start()

        dcopy((1 - y) * NZ + z, c, 0).start()

        @pl.when(first)
        def _():
            xcopy(0, p_zp, yz).start()

        @pl.when(last)
        def _():
            xcopy(1, p_zm, yz).start()

        hr = preu.shape[0] // 128 * 128

        def hidden(r):
            get = pltpu.make_async_copy(
                pre_ref.at[pl.ds(pl.multiple_of(r * hr, hr), hr)], preu.at[pl.ds(0, hr)], lsem.at[3]
            )
            get.start()
            get.wait()

            def part(n):
                p = preu[pl.ds(0, hr), cols(n, 128)].astype(F32)
                th = jnp.tanh(ROOT * (p + CUBE * (p * p * p)))
                h = (p * (0.5 * (1.0 + th))).astype(BF16)
                hidt[cols(n, 128), cols(r, hr)] = h.T

            loop(ff // 128, part)

        loop(total // hr, hidden)
        put_dy.wait()
        put_x.wait()
        w_load.wait()

        o1 = jnp.where(z == 0, 1, z - 1)
        o2 = jnp.where(z == NZ - 1, 1, jnp.where(z == 2, 3, 2))
        o3 = jnp.where(z < 2, 3, 0)

        def unit(i):
            @pl.when(i == 1)
            def _():
                pass_back(o1)

                @pl.when(z == 1)
                def _():
                    xcopy(0, p_zp, yz).start()

            @pl.when(i == 2)
            def _():
                @pl.when(inner)
                def _():
                    pass_back(o2)

                @pl.when(z == 2)
                def _():
                    xcopy(1, p_zm, yz).start()

                pass_other(z)

            @pl.when((i == 3) & edge)
            def _():
                pass_back(o2)

            @pl.when(i == 4)
            def _():
                pass_other(o1)

            @pl.when(i == 5)
            def _():
                @pl.when(inner)
                def _():
                    pass_back(o3)

                pass_other(o2)

            @pl.when(i == 6)
            def _():
                @pl.when(inner)
                def _():
                    xcopy(0, p_zp, yz - 1).wait_recv()
                    xcopy(1, p_zm, yz + 1).wait_recv()

                move_x(0)
                step_out()
                move_x(1)
                step_out()

            @pl.when(i == 7)
            def _():
                for v in (2, 3):
                    step_in()
                    move_x(v)
                    step_out()

                @pl.when(edge)
                def _():
                    pass_back(o3)

                pass_other(o3)
                step_in()
                move_x(4)
                step_out()

            row = jnp.where((i == 0) | (i == 1) | (i == 3) | (i == 6), y, 1 - y)
            near = jnp.where((i == 0) | (i == 2), z, o1)
            u = row * NZ + jnp.where(i > 5, o3, jnp.where((i == 3) | (i == 5), o2, near))
            loop(nch, lambda q: dcopy(u, 1 - c, q).wait_recv())
            get = pltpu.make_async_copy(fdy_ref.at[u], dyu, lsem.at[1])
            get_pre = pltpu.make_async_copy(
                pre_ref.at[pl.ds(pl.multiple_of(u * (NC * rows), NC * rows), NC * rows)],
                preu.at[pl.ds(0, NC * rows)], lsem.at[3],
            )
            get.start()
            get_pre.start()
            get.wait()
            get_pre.wait()

            def part(n):
                @pl.when(i == 0)
                def _():
                    pass_row(o1, n)

                @pl.when(((i == 1) & inner) | ((i == 2) & edge))
                def _():
                    pass_row(o2, n)

                @pl.when((i == 4) & inner)
                def _():
                    pass_row(o3, n)

                early = (nch - 1) // 2

                @pl.when((i == 4) & edge & (n > 0) & (n % 2 == 0))
                def _():
                    pass_row(o3, n // 2 - 1)

                @pl.when((i == 5) & edge & (n % 2 == 0))
                def _():
                    pass_row(o3, early + n // 2)

                acc = lax.dot_general(
                    dyu[...].reshape(NC * rows, d), wdn[cols(n, fn), :], (((1,), (1,)), ((), ())),
                    preferred_element_type=F32,
                )
                p = preu[pl.ds(0, NC * rows), cols(n, fn)].astype(F32)
                pp = p * p
                th = jnp.tanh(ROOT * (p + CUBE * (p * pp)))
                slope = 0.5 * (1.0 + th) + (0.5 * p) * (1.0 - th * th) * (ROOT * (1.0 + 3.0 * CUBE * pp))
                dpre[u, :, :, cols(n, fn)] = (acc * slope).astype(BF16).reshape(NC, rows, fn)

            loop(nch, part)

        loop(NY * NZ, unit)

        def sent(q):
            def block(zb):
                @pl.when((zb <= z) & (z < NZ - 1))
                def _():
                    zcopy(y, zb, q, 1).wait_send()

                @pl.when((zb >= z) & (z > 0))
                def _():
                    zcopy(y, zb, q, -1).wait_send()

                @pl.when(q == 0)
                def _():
                    @pl.when((zb <= z) & (z < NZ - 1))
                    def _():
                        zcopy(1 - y, zb, q, 1).wait_send()

                    @pl.when((zb >= z) & (z > 0))
                    def _():
                        zcopy(1 - y, zb, q, -1).wait_send()

                @pl.when((q > 0) | (zb == z))
                def _():
                    ycopy(y, zb, q).wait_send()

            loop(NZ, block)
            loop(NY * NZ, lambda b: dcopy(b, c, q).wait_send())

        loop(nch, sent)

        @pl.when(z < 2)
        def _():
            xcopy(0, p_zp, yz).wait_send()

        @pl.when(z >= 2)
        def _():
            xcopy(1, p_zm, yz).wait_send()

    pl.run_scoped(
        phase1,
        pltpu.VMEM((ff, d), BF16),
        pltpu.VMEM((NC, rows, d), BF16),
        pltpu.VMEM((max(NC * rows, 128), ff), BF16),
    )

    def phase2(own, out_r, out_l, out_d, out_y, out_w, out_e, wt, dyt, xt, odn, oin, odx, ls):
        steps = nt + TAIL

        def rcopy(slot, k):
            return remote(out_r.at[slot, k], in_r.at[slot, k], s_r.at[slot, k], r_r.at[slot, k], p_zp)

        def lcopy(slot, k):
            return remote(out_l.at[slot, k], in_l.at[slot, k], s_l.at[slot, k], r_l.at[slot, k], p_zm)

        def dsum(slot):
            return remote(out_d.at[slot], in_d.at[slot], s_d.at[slot], r_d.at[slot], p_d)

        def ysum(slot):
            return remote(out_y.at[slot], in_y.at[slot], s_y.at[slot], r_y.at[slot], p_y)

        def add_core(s):
            j = s - 1

            @pl.when(inside(j))
            def _():
                slot, ring = j % RING, j % OWN
                dsum(slot).wait_recv()

                def piece(b):
                    own[ring, b // NZ, b % NZ] += in_d[slot, b].astype(F32)

                loop(NY * NZ, piece)

        def along(s, away, start, copy, inb, outb):
            behind = z if away == 1 else NZ - 1 - z
            j = s - 1 - behind

            @pl.when(inside(j))
            def _():
                slot, ring = j % RING, j % OWN
                swaps = j % 2 == 0
                for k in range(NZ - 1, 0, -1):
                    zz = z + away * k
                    here = (zz >= 0) & (zz < NZ)
                    if k == 1:
                        here = here & jnp.logical_not(start & swaps)

                    @pl.when(here)
                    def _():
                        @pl.when(j >= RING)
                        def _():
                            copy(slot, k - 1).wait_send()

                        @pl.when(start)
                        def _():
                            def piece(h):
                                outb[slot, k - 1, h] = own[ring, h, zz].astype(BF16)

                            loop(NY, piece)

                        if k < NZ - 1:

                            @pl.when(jnp.logical_not(start))
                            def _():
                                copy(slot, k).wait_recv()

                                def piece(h):
                                    outb[slot, k - 1, h] = (own[ring, h, zz] + inb[slot, k, h].astype(F32)).astype(BF16)

                                loop(NY, piece)

                        copy(slot, k - 1).start()

        def settle(s, away, copy, inb):
            behind = z if away == 1 else NZ - 1 - z
            j = s - behind - jnp.where(behind == NZ - 1, 1, 2)

            @pl.when(inside(j) & ((behind > 1) | ((behind == 1) & (j % 2 == 1))))
            def _():
                slot, ring = j % RING, j % OWN
                copy(slot, 0).wait_recv()

                def piece(h):
                    own[ring, h, z] += inb[slot, 0, h].astype(F32)

                loop(NY, piece)

        nxt = jnp.where(first, 1, NZ - 2)
        p_nxt = jnp.where(first, p_zp, p_zm)
        p_end = jnp.where(z == 1, p_zm, p_zp)

        def wcopy(slot):
            return remote(out_w.at[slot], in_w.at[slot], s_w.at[slot], r_w.at[slot], p_y)

        def ecopy(slot, to):
            return remote(out_e.at[slot], in_e.at[slot], s_e.at[slot], r_e.at[slot], to)

        def swap(s):
            def at(j, where, body):
                @pl.when(inside(j) & (j % 2 == 0) & where)
                def _():
                    body(j % RING, j % OWN, j >= RING)

            def give(slot, ring, again):
                @pl.when(again)
                def _():
                    wcopy(slot).wait_send()

                out_w[slot] = own[ring, 1 - y, nxt].astype(BF16)
                wcopy(slot).start()

            def join(slot, ring, again):
                @pl.when(again)
                def _():
                    ecopy(slot, p_nxt).wait_send()

                wcopy(slot).wait_recv()
                out_e[slot] = (own[ring, y, nxt] + in_w[slot].astype(F32)).astype(BF16)
                ecopy(slot, p_nxt).start()

            def take(slot, ring, again):
                ecopy(slot, p_end).wait_recv()
                own[ring, y, z] += in_e[slot].astype(F32)

            at(s - 1, edge, give)
            at(s - 3, edge, join)
            at(s - 4, inner, take)

        def across(s):
            j = s - 4

            @pl.when(inside(j))
            def _():
                slot, ring = j % RING, j % OWN

                @pl.when(j >= RING)
                def _():
                    ysum(slot).wait_send()

                out_y[slot] = own[ring, 1 - y, z].astype(BF16)
                ysum(slot).start()

        def put_dx(j):
            return pltpu.make_async_copy(odx.at[j % 2], dx_ref.at[:, cols(j, tn)], ls.at[5, j % 2])

        def finish(s):
            j = s - 6

            @pl.when(inside(j))
            def _():
                slot, ring = j % RING, j % OWN

                @pl.when(j >= 2)
                def _():
                    put_dx(j - 2).wait()

                ysum(slot).wait_recv()
                odx[j % 2] = (own[ring, y, z] + in_y[slot].astype(F32)).astype(BF16)
                put_dx(j).start()

        def get_x(j):
            return pltpu.make_async_copy(fx_ref.at[:, :, :, cols(j, tn)], xt.at[j % 2], ls.at[2, j % 2])

        def get_w(j):
            return pltpu.make_async_copy(win_ref.at[cols(j, tn)], wt.at[j % 2], ls.at[0, j % 2])

        def get_dy(j):
            return pltpu.make_async_copy(fdy_ref.at[:, :, :, cols(j, tn)], dyt.at[j % 2], ls.at[1, j % 2])

        def put_dn(j):
            return pltpu.make_async_copy(odn.at[j % 2], dwdn_ref.at[:, cols(j, tn)], ls.at[3, j % 2])

        def put_in(j):
            return pltpu.make_async_copy(oin.at[j % 2], dwin_ref.at[cols(j, tn)], ls.at[4, j % 2])

        def term(j):
            slot, ring = j % RING, j % OWN
            get_w(j).wait()

            @pl.when(j + 1 < nt)
            def _():
                get_w(j + 1).start()

            @pl.when(j >= RING)
            def _():
                dsum(slot).wait_send()

            def dot(core, h):
                lhs = dpre[h * NZ : (h + 1) * NZ, core].reshape(NZ * rows, ff)
                return lax.dot_general(
                    lhs, wt[j % 2], (((1,), (1,)), ((), ())), preferred_element_type=F32
                ).reshape(NZ, rows, tn)

            for h in range(NY):
                out_d[slot, h * NZ : (h + 1) * NZ] = dot(1 - c, h).astype(BF16)
            dsum(slot).start()
            for h in range(NY):
                own[ring, h] = dot(c, h)

        def down(j):
            get_dy(j).wait()

            @pl.when(j + 1 < nt)
            def _():
                get_dy(j + 1).start()

            @pl.when(j >= 2)
            def _():
                put_dn(j - 2).wait()

            rhs = dyt[j % 2].reshape(total, tn)
            for m in range(0, ff, ff // 4):
                odn[j % 2, m : m + ff // 4] = jnp.dot(
                    hidt[m : m + ff // 4], rhs, preferred_element_type=F32
                ).astype(BF16)
            put_dn(j).start()

        def inward(j):
            get_x(j).wait()

            @pl.when(j >= 2)
            def _():
                put_in(j - 2).wait()

            lhs = xt[j % 2].reshape(total, tn)
            for n in range(0, ff, ff // 2):
                oin[j % 2, :, n : n + ff // 2] = lax.dot_general(
                    lhs, dpre[:, :, :, n : n + ff // 2].reshape(total, ff // 2), (((0,), (0,)), ((), ())),
                    preferred_element_type=F32,
                ).astype(BF16)
            put_in(j).start()

        get_w(0).start()
        get_dy(0).start()

        def step(s):
            step_in()
            add_core(s)
            swap(s)
            along(s, 1, first, rcopy, in_r, out_r)
            along(s, -1, last, lcopy, in_l, out_l)
            settle(s, 1, rcopy, in_r)
            settle(s, -1, lcopy, in_l)
            across(s)
            finish(s)
            move_x(s + LEAD)

            @pl.when(s < steps - WINDOW)
            def _():
                step_out()

            @pl.when(s < nt)
            def _():
                term(s)

            @pl.when(inside(s - 1))
            def _():
                xd(s - 1, 1 - c).wait_recv()
                get_x(s - 1).start()

            m = s - (s + 1) // 8

            @pl.when(((s + 1) % 8 != 0) & (m < nt))
            def _():
                down(m)

            @pl.when(inside(s - 1))
            def _():
                inward(s - 1)

        loop(steps, step)
        loop(2, lambda i: finish(steps + i))

        for j in range(nt - RING, nt):
            slot = j % RING
            for k in range(NZ - 1):
                swapped = k == 0 and j % 2 == 0

                @pl.when((z + k + 1 < NZ) & jnp.logical_not(first & swapped))
                def _():
                    rcopy(slot, k).wait_send()

                @pl.when((z - k - 1 >= 0) & jnp.logical_not(last & swapped))
                def _():
                    lcopy(slot, k).wait_send()

            if j % 2 == 0:

                @pl.when(edge)
                def _():
                    wcopy(slot).wait_send()
                    ecopy(slot, p_nxt).wait_send()

            dsum(slot).wait_send()
            ysum(slot).wait_send()
            xy(j, y).wait_send()
            xd(j, c).wait_send()
            x_out(j, 1, True)
            x_out(j, -1, True)

            @pl.when(z == 2)
            def _():
                xz(j, 1, 1, 0).wait_send()

            @pl.when(z == 1)
            def _():
                xz(j, -1, 1, NZ - 1).wait_send()

        for j in range(nt - 2, nt):
            put_dn(j).wait()
            put_in(j).wait()
            put_dx(j).wait()

    pl.run_scoped(
        phase2,
        pltpu.VMEM((OWN, NY, NZ, rows, tn), F32),
        pltpu.VMEM((RING, NZ - 1, NY, rows, tn), BF16),
        pltpu.VMEM((RING, NZ - 1, NY, rows, tn), BF16),
        pltpu.VMEM((RING, NY * NZ, rows, tn), BF16),
        pltpu.VMEM((RING, rows, tn), BF16),
        pltpu.VMEM((RING, rows, tn), BF16),
        pltpu.VMEM((RING, rows, tn), BF16),
        pltpu.VMEM((2, tn, ff), BF16),
        pltpu.VMEM((2, NY * NZ, NC, rows, tn), BF16),
        pltpu.VMEM((2, NY * NZ, NC, rows, tn), BF16),
        pltpu.VMEM((2, ff, tn), BF16),
        pltpu.VMEM((2, tn, ff), BF16),
        pltpu.VMEM((2, rows, tn), BF16),
        pltpu.SemaphoreType.DMA((6, 2)),
    )


def call(rows, d, ff, tn, nch, fn, x, dy, pre, win, wdn):
    blocks = NY * NZ
    total = blocks * NC * rows
    dma = pltpu.SemaphoreType.DMA
    any_ = pl.BlockSpec(memory_space=pl.ANY)
    return pl.pallas_call(
        functools.partial(bwd_kernel, (rows, d, ff, tn, nch, fn)),
        name="bwd",
        out_shape=[
            jax.ShapeDtypeStruct((rows, d), BF16),
            jax.ShapeDtypeStruct((d, ff), BF16),
            jax.ShapeDtypeStruct((ff, d), BF16),
            jax.ShapeDtypeStruct((blocks, NC, rows, d), BF16),
            jax.ShapeDtypeStruct((blocks, NC, rows, d), BF16),
        ],
        in_specs=[any_] * 5,
        out_specs=[any_] * 5,
        scratch_shapes=[
            pltpu.VMEM((blocks, NC, rows, ff), BF16),
            pltpu.VMEM((ff, total), BF16),
            pltpu.VMEM((RING, NZ - 1, NY, rows, tn), BF16),
            pltpu.VMEM((RING, NZ - 1, NY, rows, tn), BF16),
            pltpu.VMEM((RING, blocks, rows, tn), BF16),
            pltpu.VMEM((RING, rows, tn), BF16),
            pltpu.VMEM((RING, rows, tn), BF16),
            pltpu.VMEM((RING, rows, tn), BF16),
            dma((NZ, nch + 1)), dma((NZ, nch)), dma((blocks, nch)),
            dma((NZ, nch + 1)), dma((NZ, nch + 1)), dma((NZ, nch)), dma((blocks, nch)),
            dma((2,)), dma((2,)), dma((4,)),
            dma((RING, NZ - 1)), dma((RING, NZ - 1)), dma((RING,)), dma((RING,)), dma((RING,)), dma((RING,)),
            dma((RING, NZ - 1)), dma((RING, NZ - 1)), dma((RING,)), dma((RING,)), dma((RING,)), dma((RING,)),
            dma((2, 2, RING)), dma((2, 2, RING)), dma((RING,)), dma((RING,)), dma((RING,)), dma((RING,)),
            pltpu.SemaphoreType.REGULAR((4,)),
        ],
        compiler_params=pltpu.CompilerParams(
            collective_id=0, has_side_effects=True, vmem_limit_bytes=67043328
        ),
    )(x, dy, pre, win, wdn)


def solution(mesh):
    spec = jax.sharding.PartitionSpec
    rows_of, cols_of = spec(("dp", "tp"), None), spec("dp", "tp")

    def local(x, dy, pre, win, wdn):
        rows, d = x.shape
        ff = pre.shape[1]
        dx, dwin, dwdn, _, _ = call(rows, d, ff, 256, 7, 256, x, dy, pre, win, wdn)
        return dx, dwin, dwdn

    return jax.shard_map(
        local,
        mesh=mesh,
        in_specs=(rows_of, rows_of, cols_of, spec(None, "tp"), spec("tp", None)),
        out_specs=(rows_of, cols_of, rows_of),
        check_vma=False,
    )
```

time: 596 us -> 539 us (0.904)
  Pallas kernels: 556 us -> 501 us
    pallas_call x1, Pallas kernels: 556 us -> 501 us  [call(): pl.pallas_call(functools.partial(bwd_kernel, (rows, d, ff, tn, nch, fn)),...]
where the time goes in v2:
time: 539 us
  Pallas kernels  501 us (93%)
  local copies, waits for them, and re-layouts  36.8 us (7%)
    pallas_call x1, Pallas kernels, call(): pl.pallas_call(functools.partial(bwd_kernel, (rows, d, ff, tn, nch, fn)),...  501 us
    unnamed x17, local copies, waits for them, and re-layouts  36.8 us

profile of v2, /device:TPU:0, one launch (start us, length us, event | category | flops | bytes accessed | tf_op | source)
XLA Modules:
  0.0 538.7 jit_solution(8923100278569535609)
XLA Ops:
  0.6 501.2 %bwd.1 = (bf16[160,7168]{1,0:T(8,128)(2,1)}, bf16[7168,1792]{1,0:T(8,128)(2,1)}, bf16[1792,7168]{1,0:T(8,128)(2,1)}, bf16[8,2,160,7168]{3,2,1,0:T(8,128)(2,1)}, bf16[8,2,160,7168]{3,2,1,0:T(8,128)(2,1)}) custom-call(bf16[160,7168]{1,0:T(8,128)(2,1)} %x_ref.1, bf16[160,7168]{1,0:T(8,128)(2,1)} %dy_ref.1, bf16[2560,1792]{1,0:T(8,128)(2,1)} %pre_ref.1, ...), custom_call_target="tpu_custom_call" | custom-call | tf_op jit(solution)/shard_map/bwd/pallas_call | solution.py:811
  501.8 0.0 slice-start
  501.8 3.3 copy.11
  505.2 0.0 slice-start.1
  505.2 0.0 slice-start.2
  505.2 0.0 slice-start.3
  505.2 0.0 slice-start.4
  505.2 0.0 slice-start.5
  505.2 0.0 slice-start.6
  505.2 24.4 %copy.12 = bf16[7168,1792]{1,0:T(8,128)(2,1)} copy(bf16[7168,1792]{1,0:T(8,128)(2,1)} %get-tuple-element.13) | data formatting | bytes 51380224
  529.6 0.0 slice-done
  529.6 0.0 slice-done.1
  529.6 0.0 slice-done.2
  529.6 0.0 slice-done.3
  529.6 0.0 slice-done.4
  529.6 0.0 slice-done.5
  529.6 0.0 slice-done.6
  529.6 9.1 %copy.13 = bf16[1792,7168]{1,0:T(8,128)(2,1)} copy(bf16[1792,7168]{1,0:T(8,128)(2,1)S(1)} %bitcast.1) | data formatting | bytes 51380224
  (1 shorter events, 0.0 us)
Async XLA Ops:
  501.8 27.8 %slice-start = ((s8[25690112]{0:T(1024)(128)(4,1)}), s8[4194304]{0:T(1024)(128)(4,1)S(1)}, s32[]{:S(2)}) async-start(s8[25690112]{0:T(1024)(128)(4,1)} %bitcast), calls=%async_computation | async-start | bytes 8388608
  505.2 24.4 %slice-start.1 = ((s8[25690112]{0:T(1024)(128)(4,1)}), s8[4194304]{0:T(1024)(128)(4,1)S(1)}, s32[]{:S(2)}) async-start(s8[25690112]{0:T(1024)(128)(4,1)} %bitcast), calls=%async_computation.1 | async-start | bytes 8388608
  505.2 24.4 %slice-start.2 = ((s8[25690112]{0:T(1024)(128)(4,1)}), s8[4194304]{0:T(1024)(128)(4,1)S(1)}, s32[]{:S(2)}) async-start(s8[25690112]{0:T(1024)(128)(4,1)} %bitcast), calls=%async_computation.2 | async-start | bytes 8388608
  505.2 24.4 %slice-start.3 = ((s8[25690112]{0:T(1024)(128)(4,1)}), s8[4194304]{0:T(1024)(128)(4,1)S(1)}, s32[]{:S(2)}) async-start(s8[25690112]{0:T(1024)(128)(4,1)} %bitcast), calls=%async_computation.3 | async-start | bytes 8388608
  505.2 24.4 %slice-start.4 = ((s8[25690112]{0:T(1024)(128)(4,1)}), s8[4194304]{0:T(1024)(128)(4,1)S(1)}, s32[]{:S(2)}) async-start(s8[25690112]{0:T(1024)(128)(4,1)} %bitcast), calls=%async_computation.4 | async-start | bytes 8388608
  505.2 24.4 %slice-start.5 = ((s8[25690112]{0:T(1024)(128)(4,1)}), s8[4194304]{0:T(1024)(128)(4,1)S(1)}, s32[]{:S(2)}) async-start(s8[25690112]{0:T(1024)(128)(4,1)} %bitcast), calls=%async_computation.5 | async-start | bytes 8388608
  505.2 24.4 %slice-start.6 = ((s8[25690112]{0:T(1024)(128)(4,1)}), s8[524288]{0:T(1024)(128)(4,1)S(1)}, s32[]{:S(2)}) async-start(s8[25690112]{0:T(1024)(128)(4,1)} %bitcast), calls=%async_computation.6 | async-start | bytes 1048576

commit v3 on v2

--- a/solution.py
+++ b/solution.py
@@ -13,9 +13,42 @@
 OWN = 6
 WINDOW = 2
 TAIL = 4
+SLACK = 12.0
 LEAD = 5
 ROOT = 0.7978845608028654
 CUBE = 0.044715
+
+
+def relays(inner, n):
+    block = 50.0
+    chunk = block / n
+    due = {}
+    for q in range(n):
+        here = (q + 1) * chunk
+        due[0, q] = -1.0
+        due[1, q] = due[2, q] = here
+        due[3, q] = here if inner else block + 2 * chunk + here
+        due[4, q] = block + here - chunk if q else block + 2 * chunk
+        due[5, q] = 2 * block - chunk + here - chunk if q else 2.4 * chunk + (block if inner else 2 * block)
+        due[6, q] = (block + 2 * chunk if inner else 2 * block + 3 * chunk) + here
+        due[7, q] = 3 * block - 2 * chunk + here - chunk if q else 2.4 * chunk + (2 * block if inner else 3 * block + chunk)
+    for i, q in due:
+        if i in (4, 5, 7) and q:
+            due[i, q] += SLACK
+    order = sorted(due, key=lambda k: (due[k], k[1], k[0]))
+    first, last = {}, {}
+    for e, (i, _) in enumerate(order):
+        first.setdefault(i, e)
+        last[i] = e
+    codes, keep, free = [], {}, [2, 1, 0]
+    for e, (i, q) in enumerate(order):
+        if e == first[i]:
+            keep[i] = free.pop()
+        mark = (e == first[i]) + 2 * (e == last[i])
+        codes.append(((i * 16 + q) * 4 + mark) * 4 + keep[i])
+        if e == last[i]:
+            free.append(keep[i])
+    return codes
 
 
 def bwd_kernel(
@@ -23,7 +56,7 @@
     x_ref, dy_ref, pre_ref, win_ref, wdn_ref,
     dx_ref, dwin_ref, dwdn_ref, fx_ref, fdy_ref,
     dpre, hidt, in_r, in_l, in_d, in_y, in_w, in_e,
-    rz, ry, rd, szp, szm, sy, sd, rx, sx, lsem,
+    rz, ry, rd, szp, szm, sy, sd, rx, sx, lsem, ls1, ls2,
     r_r, r_l, r_d, r_y, r_w, r_e, s_r, s_l, s_d, s_y, s_w, s_e,
     rxz, sxz, rxy, sxy, rxd, sxd, cred,
 ):
@@ -209,229 +242,251 @@
     def xcopy(k, to, b):
         return remote(x_ref, fx_ref.at[b, c], sx.at[k], rx.at[k], to)
 
-    def phase1(wdn, dyu, preu):
+    def phase1(wdn):
         w_load = pltpu.make_async_copy(wdn_ref, wdn, lsem.at[0])
-        own_dy = pltpu.make_async_copy(dy_ref, dyu.at[c], lsem.at[1])
-        own_x = pltpu.make_async_copy(x_ref, dyu.at[1 - c], lsem.at[2])
-        own_dy.start()
-        own_x.start()
-
-        def send_own(q):
-            src = dy_ref.at[:, cols(q, ck)]
-
-            @pl.when(jnp.logical_not(last))
-            def _():
-                zcopy(y, z, q, 1, src).start()
-
-            @pl.when(jnp.logical_not(first))
-            def _():
-                zcopy(y, z, q, -1, src).start()
-
-            ycopy(y, z, q, src).start()
-            dcopy(yz, c, q, src).start()
-
-        loop(nch, send_own)
-        own_dy.wait()
-        own_x.wait()
-        put_dy = pltpu.make_async_copy(dyu.at[c], fdy_ref.at[yz, c], lsem.at[1])
-        put_x = pltpu.make_async_copy(dyu.at[1 - c], fx_ref.at[yz, c], lsem.at[2])
-        put_dy.start()
-        put_x.start()
-        w_load.start()
-
-        def pass_z(row, zb, q):
-            @pl.when((zb < z) & (z < NZ - 1))
-            def _():
-                zcopy(row, zb, q, 1).start()
-
-            @pl.when((zb > z) & (z > 0))
-            def _():
-                zcopy(row, zb, q, -1).start()
-
-        def pass_row(zb, q):
-            zcopy(y, zb, q, 1).wait_recv()
-            pass_z(y, zb, q)
-
-            @pl.when(q > 0)
-            def _():
-                ycopy(y, zb, q).start()
-
-            dcopy(y * NZ + zb, c, q).start()
-
-        def pass_back(zb):
-            zcopy(1 - y, zb, 0, 1).wait_recv()
-            pass_z(1 - y, zb, 0)
-            dcopy((1 - y) * NZ + zb, c, 0).start()
-
-        def pass_other(zb):
-            def piece(q):
-                ycopy(1 - y, zb, q + 1).wait_recv()
-                dcopy((1 - y) * NZ + zb, c, q + 1).start()
-
-            loop(nch - 1, piece)
-
-        ycopy(1 - y, z, 0).wait_recv()
-
-        @pl.when(jnp.logical_not(last))
-        def _():
-            zcopy(1 - y, z, 0, 1).start()
-
-        @pl.when(jnp.logical_not(first))
-        def _():
-            zcopy(1 - y, z, 0, -1).start()
-
-        dcopy((1 - y) * NZ + z, c, 0).start()
-
-        @pl.when(first)
-        def _():
-            xcopy(0, p_zp, yz).start()
-
-        @pl.when(last)
-        def _():
-            xcopy(1, p_zm, yz).start()
-
-        hr = preu.shape[0] // 128 * 128
-
-        def hidden(r):
-            get = pltpu.make_async_copy(
-                pre_ref.at[pl.ds(pl.multiple_of(r * hr, hr), hr)], preu.at[pl.ds(0, hr)], lsem.at[3]
-            )
-            get.start()
-            get.wait()
-
-            def part(n):
-                p = preu[pl.ds(0, hr), cols(n, 128)].astype(F32)
-                th = jnp.tanh(ROOT * (p + CUBE * (p * p * p)))
-                h = (p * (0.5 * (1.0 + th))).astype(BF16)
-                hidt[cols(n, 128), cols(r, hr)] = h.T
-
-            loop(ff // 128, part)
-
-        loop(total // hr, hidden)
-        put_dy.wait()
-        put_x.wait()
+
+        def start(bounce, part_of_pre):
+            own_dy = pltpu.make_async_copy(dy_ref, bounce.at[0], lsem.at[1])
+            own_x = pltpu.make_async_copy(x_ref, bounce.at[1], lsem.at[2])
+            own_dy.start()
+            own_x.start()
+
+            def send_own(q):
+                src = dy_ref.at[:, cols(q, ck)]
+
+                @pl.when(jnp.logical_not(last))
+                def _():
+                    zcopy(y, z, q, 1, src).start()
+
+                @pl.when(jnp.logical_not(first))
+                def _():
+                    zcopy(y, z, q, -1, src).start()
+
+                ycopy(y, z, q, src).start()
+                dcopy(yz, c, q, src).start()
+
+            loop(nch, send_own)
+
+            hr = part_of_pre.shape[1]
+
+            def get(r):
+                return pltpu.make_async_copy(
+                    pre_ref.at[pl.ds(pl.multiple_of(r * hr, hr), hr)], part_of_pre.at[r % 2], ls1.at[r % 2]
+                )
+
+            get(0).start()
+            own_dy.wait()
+            own_x.wait()
+            put_dy = pltpu.make_async_copy(bounce.at[0], fdy_ref.at[yz, c], lsem.at[1])
+            put_x = pltpu.make_async_copy(bounce.at[1], fx_ref.at[yz, c], lsem.at[2])
+            put_dy.start()
+            put_x.start()
+            w_load.start()
+
+            def hidden(r):
+                get(r).wait()
+
+                @pl.when(r + 1 < total // hr)
+                def _():
+                    get(r + 1).start()
+
+                def part(n):
+                    p = part_of_pre[r % 2, :, cols(n, hw)].astype(F32)
+                    th = jnp.tanh(ROOT * (p + CUBE * (p * p * p)))
+                    h = (p * (0.5 * (1.0 + th))).astype(BF16)
+                    hidt[cols(n, hw), cols(r, hr)] = h.T
+
+                hw = 256 if ff % 256 == 0 else 128
+                loop(ff // hw, part)
+
+            loop(total // hr, hidden)
+            put_dy.wait()
+            put_x.wait()
+
+        pl.run_scoped(
+            start, pltpu.VMEM((2, rows, d), BF16), pltpu.VMEM((2, 256 if total % 256 == 0 else 128, ff), BF16)
+        )
         w_load.wait()
 
         o1 = jnp.where(z == 0, 1, z - 1)
         o2 = jnp.where(z == NZ - 1, 1, jnp.where(z == 2, 3, 2))
         o3 = jnp.where(z < 2, 3, 0)
 
-        def unit(i):
-            @pl.when(i == 1)
-            def _():
-                pass_back(o1)
-
-                @pl.when(z == 1)
+        def pass_z(row, zb, q):
+            @pl.when((zb < z) & (z < NZ - 1))
+            def _():
+                zcopy(row, zb, q, 1).start()
+
+            @pl.when((zb > z) & (z > 0))
+            def _():
+                zcopy(row, zb, q, -1).start()
+
+        def chip(i):
+            row = jnp.where((i == 0) | (i == 1) | (i == 3) | (i == 6), y, 1 - y)
+            near = jnp.where((i == 0) | (i == 2), z, o1)
+            return row, jnp.where(i > 5, o3, jnp.where((i == 3) | (i == 5), o2, near))
+
+        def unpack(code):
+            return code // 256, code // 16 % 16, code // 4 % 4, code % 4
+
+        def relay(code):
+            i, q, _, _ = unpack(code)
+            row, zb = chip(i)
+
+            @pl.when((i > 0) & (row == y))
+            def _():
+                zcopy(y, zb, q, 1).wait_recv()
+                pass_z(y, zb, q)
+
+                @pl.when(q > 0)
+                def _():
+                    ycopy(y, zb, q).start()
+
+            @pl.when((row != y) & (q == 0) & (i == 2))
+            def _():
+                ycopy(1 - y, z, 0).wait_recv()
+
+                @pl.when(jnp.logical_not(last))
+                def _():
+                    zcopy(1 - y, z, 0, 1).start()
+
+                @pl.when(jnp.logical_not(first))
+                def _():
+                    zcopy(1 - y, z, 0, -1).start()
+
+                @pl.when(first)
                 def _():
                     xcopy(0, p_zp, yz).start()
 
-            @pl.when(i == 2)
-            def _():
-                @pl.when(inner)
-                def _():
-                    pass_back(o2)
-
-                @pl.when(z == 2)
+                @pl.when(last)
                 def _():
                     xcopy(1, p_zm, yz).start()
 
-                pass_other(z)
-
-            @pl.when((i == 3) & edge)
-            def _():
-                pass_back(o2)
-
-            @pl.when(i == 4)
-            def _():
-                pass_other(o1)
-
-            @pl.when(i == 5)
-            def _():
-                @pl.when(inner)
-                def _():
-                    pass_back(o3)
-
-                pass_other(o2)
-
-            @pl.when(i == 6)
-            def _():
-                @pl.when(inner)
-                def _():
-                    xcopy(0, p_zp, yz - 1).wait_recv()
-                    xcopy(1, p_zm, yz + 1).wait_recv()
-
-                move_x(0)
-                step_out()
-                move_x(1)
-                step_out()
-
-            @pl.when(i == 7)
-            def _():
-                for v in (2, 3):
+            @pl.when((row != y) & (q == 0) & (i != 2))
+            def _():
+                zcopy(1 - y, zb, 0, 1).wait_recv()
+                pass_z(1 - y, zb, 0)
+
+                @pl.when((i == 4) & (z == 1))
+                def _():
+                    xcopy(0, p_zp, yz).start()
+
+                @pl.when((i == 5) & (z == 2))
+                def _():
+                    xcopy(1, p_zm, yz).start()
+
+            @pl.when((row != y) & (q > 0))
+            def _():
+                @pl.when((i == 7) & (q == nch - 3 + (nch < 4)))
+                def _():
+                    @pl.when(inner)
+                    def _():
+                        xcopy(0, p_zp, yz - 1).wait_recv()
+                        xcopy(1, p_zm, yz + 1).wait_recv()
+
+                    for v in range(WINDOW):
+                        move_x(v)
+                        step_out()
+
+                ycopy(1 - y, zb, q).wait_recv()
+
+            @pl.when(i > 0)
+            def _():
+                dcopy(row * NZ + zb, c, q).start()
+
+            @pl.when((i == 7) & (q == nch - 1))
+            def _():
+                for v in range(WINDOW, LEAD - 1):
                     step_in()
                     move_x(v)
                     step_out()
 
-                @pl.when(edge)
-                def _():
-                    pass_back(o3)
-
-                pass_other(o3)
-                step_in()
-                move_x(4)
-                step_out()
-
-            row = jnp.where((i == 0) | (i == 1) | (i == 3) | (i == 6), y, 1 - y)
-            near = jnp.where((i == 0) | (i == 2), z, o1)
-            u = row * NZ + jnp.where(i > 5, o3, jnp.where((i == 3) | (i == 5), o2, near))
-            loop(nch, lambda q: dcopy(u, 1 - c, q).wait_recv())
-            get = pltpu.make_async_copy(fdy_ref.at[u], dyu, lsem.at[1])
-            get_pre = pltpu.make_async_copy(
-                pre_ref.at[pl.ds(pl.multiple_of(u * (NC * rows), NC * rows), NC * rows)],
-                preu.at[pl.ds(0, NC * rows)], lsem.at[3],
-            )
-            get.start()
-            get_pre.start()
-            get.wait()
-            get_pre.wait()
-
-            def part(n):
-                @pl.when(i == 0)
-                def _():
-                    pass_row(o1, n)
-
-                @pl.when(((i == 1) & inner) | ((i == 2) & edge))
-                def _():
-                    pass_row(o2, n)
-
-                @pl.when((i == 4) & inner)
-                def _():
-                    pass_row(o3, n)
-
-                early = (nch - 1) // 2
-
-                @pl.when((i == 4) & edge & (n > 0) & (n % 2 == 0))
-                def _():
-                    pass_row(o3, n // 2 - 1)
-
-                @pl.when((i == 5) & edge & (n % 2 == 0))
-                def _():
-                    pass_row(o3, early + n // 2)
-
-                acc = lax.dot_general(
-                    dyu[...].reshape(NC * rows, d), wdn[cols(n, fn), :], (((1,), (1,)), ((), ())),
-                    preferred_element_type=F32,
+        def stream(dyc, preu, acc):
+            orders = [[relays(inner_chip, nch)[e] for e in range(NY * NZ * nch)] for inner_chip in (False, True)]
+            places = len(orders[0])
+
+            def at(e):
+                code = jnp.where(inner, orders[1][0], orders[0][0])
+                for k in range(1, places):
+                    code = jnp.where(e == k, jnp.where(inner, orders[1][k], orders[0][k]), code)
+                return code
+
+            def get(code, slot):
+                i, q, _, _ = unpack(code)
+                row, zb = chip(i)
+                return pltpu.make_async_copy(
+                    fdy_ref.at[row * NZ + zb, :, :, cols(q, ck)], dyc.at[slot], ls1.at[slot]
                 )
-                p = preu[pl.ds(0, NC * rows), cols(n, fn)].astype(F32)
-                pp = p * p
-                th = jnp.tanh(ROOT * (p + CUBE * (p * pp)))
-                slope = 0.5 * (1.0 + th) + (0.5 * p) * (1.0 - th * th) * (ROOT * (1.0 + 3.0 * CUBE * pp))
-                dpre[u, :, :, cols(n, fn)] = (acc * slope).astype(BF16).reshape(NC, rows, fn)
-
-            loop(nch, part)
-
-        loop(NY * NZ, unit)
-
+
+            def fetch(code, slot):
+                i, q, _, _ = unpack(code)
+                row, zb = chip(i)
+                dcopy(row * NZ + zb, 1 - c, q).wait_recv()
+                get(code, slot).start()
+
+            def get_pre(u, keep):
+                at = pl.ds(pl.multiple_of(u * (NC * rows), NC * rows), NC * rows)
+                return pltpu.make_async_copy(pre_ref.at[at], preu.at[keep], ls2.at[keep])
+
+            def place(e, codes):
+                code, following = codes
+                later = at(e + 2)
+
+                @pl.when(e + 2 < places)
+                def _():
+                    relay(later)
+
+                @pl.when(e + 1 < places)
+                def _():
+                    fetch(following, (e + 1) % 2)
+
+                i, q, mark, keep = unpack(code)
+                row, zb = chip(i)
+                u = row * NZ + zb
+
+                @pl.when(mark % 2 == 1)
+                def _():
+                    get_pre(u, keep).start()
+
+                get(code, e % 2).wait()
+                lhs = dyc[e % 2].reshape(NC * rows, ck)
+                for n in range(0, ff, fn):
+                    term = lax.dot_general(
+                        lhs, wdn[n : n + fn, cols(q, ck)], (((1,), (1,)), ((), ())), preferred_element_type=F32
+                    )
+                    acc[keep, :, n : n + fn] = jnp.where(mark % 2 == 1, 0.0, acc[keep, :, n : n + fn]) + term
+
+                @pl.when(mark >= 2)
+                def _():
+                    get_pre(u, keep).wait()
+
+                    def part(n):
+                        p = preu[keep, :, cols(n, fn)].astype(F32)
+                        pp = p * p
+                        th = jnp.tanh(ROOT * (p + CUBE * (p * pp)))
+                        slope = 0.5 * (1.0 + th) + (0.5 * p) * (1.0 - th * th) * (ROOT * (1.0 + 3.0 * CUBE * pp))
+                        dpre[u, :, :, cols(n, fn)] = (acc[keep, :, cols(n, fn)] * slope).astype(BF16).reshape(NC, rows, fn)
+
+                    loop(ff // fn, part)
+
+                return following, later
+
+            codes = at(0), at(1)
+            relay(codes[0])
+            relay(codes[1])
+            fetch(codes[0], 0)
+            lax.fori_loop(0, places, place, codes)
+
+        pl.run_scoped(
+            stream,
+            pltpu.VMEM((2, NC, rows, ck), BF16),
+            pltpu.VMEM((3, NC * rows, ff), BF16),
+            pltpu.VMEM((3, NC * rows, ff), F32),
+        )
+
+    pl.run_scoped(phase1, pltpu.VMEM((ff, d), BF16))
+
+    def all_sent():
         def sent(q):
             def block(zb):
                 @pl.when((zb <= z) & (z < NZ - 1))
@@ -468,13 +523,6 @@
         @pl.when(z >= 2)
         def _():
             xcopy(1, p_zm, yz).wait_send()
-
-    pl.run_scoped(
-        phase1,
-        pltpu.VMEM((ff, d), BF16),
-        pltpu.VMEM((NC, rows, d), BF16),
-        pltpu.VMEM((max(NC * rows, 128), ff), BF16),
-    )
 
     def phase2(own, out_r, out_l, out_d, out_y, out_w, out_e, wt, dyt, xt, odn, oin, odx, ls):
         steps = nt + TAIL
@@ -705,6 +753,10 @@
 
         get_w(0).start()
         get_dy(0).start()
+
+        step_in()
+        move_x(LEAD - 1)
+        step_out()
 
         def step(s):
             step_in()
@@ -726,14 +778,18 @@
             def _():
                 term(s)
 
+            @pl.when(s == nt + 1)
+            def _():
+                all_sent()
+
             @pl.when(inside(s - 1))
             def _():
                 xd(s - 1, 1 - c).wait_recv()
                 get_x(s - 1).start()
 
-            m = s - (s + 1) // 8
-
-            @pl.when(((s + 1) % 8 != 0) & (m < nt))
+            m = s - s // 9 - 1
+
+            @pl.when((s % 9 != 0) & (m < nt))
             def _():
                 down(m)
 
@@ -831,7 +887,7 @@
             pltpu.VMEM((RING, rows, tn), BF16),
             dma((NZ, nch + 1)), dma((NZ, nch)), dma((blocks, nch)),
             dma((NZ, nch + 1)), dma((NZ, nch + 1)), dma((NZ, nch)), dma((blocks, nch)),
-            dma((2,)), dma((2,)), dma((4,)),
+            dma((2,)), dma((2,)), dma((3,)), dma((2,)), dma((3,)),
             dma((RING, NZ - 1)), dma((RING, NZ - 1)), dma((RING,)), dma((RING,)), dma((RING,)), dma((RING,)),
             dma((RING, NZ - 1)), dma((RING, NZ - 1)), dma((RING,)), dma((RING,)), dma((RING,)), dma((RING,)),
             dma((2, 2, RING)), dma((2, 2, RING)), dma((RING,)), dma((RING,)), dma((RING,)), dma((RING,)),

time: 539 us -> 524 us (0.972)
  Pallas kernels: 501 us -> 485 us
    pallas_call x1, Pallas kernels: 501 us -> 485 us  [call(): pl.pallas_call(functools.partial(bwd_kernel, (rows, d, ff, tn, nch, fn)),...]
where the time goes in v3:
time: 524 us; the launch traced here: 522 us
  Pallas kernels  485 us (93%)
  local copies, waits for them, and re-layouts  36.8 us (7%)
    pallas_call x1, Pallas kernels, call(): pl.pallas_call(functools.partial(bwd_kernel, (rows, d, ff, tn, nch, fn)),...  485 us
    unnamed x17, local copies, waits for them, and re-layouts  36.8 us

profile of v3, /device:TPU:0, one launch (start us, length us, event | category | flops | bytes accessed | tf_op | source)
XLA Modules:
  0.0 522.5 jit_solution(15051838319408179888)
XLA Ops:
  0.6 484.9 %bwd.1 = (bf16[160,7168]{1,0:T(8,128)(2,1)}, bf16[7168,1792]{1,0:T(8,128)(2,1)}, bf16[1792,7168]{1,0:T(8,128)(2,1)}, bf16[8,2,160,7168]{3,2,1,0:T(8,128)(2,1)}, bf16[8,2,160,7168]{3,2,1,0:T(8,128)(2,1)}) custom-call(bf16[160,7168]{1,0:T(8,128)(2,1)} %x_ref.1, bf16[160,7168]{1,0:T(8,128)(2,1)} %dy_ref.1, bf16[2560,1792]{1,0:T(8,128)(2,1)} %pre_ref.1, ...), custom_call_target="tpu_custom_call" | custom-call | tf_op jit(solution)/shard_map/bwd/pallas_call | solution.py:867
  485.6 0.0 slice-start
  485.6 3.3 copy.11
  488.9 0.0 slice-start.1
  488.9 0.0 slice-start.2
  488.9 0.0 slice-start.3
  488.9 0.0 slice-start.4
  488.9 0.0 slice-start.5
  488.9 0.0 slice-start.6
  488.9 24.4 %copy.12 = bf16[7168,1792]{1,0:T(8,128)(2,1)} copy(bf16[7168,1792]{1,0:T(8,128)(2,1)} %get-tuple-element.13) | data formatting | bytes 51380224
  513.3 0.0 slice-done
  513.3 0.0 slice-done.1
  513.3 0.0 slice-done.2
  513.3 0.0 slice-done.3
  513.3 0.0 slice-done.4
  513.3 0.0 slice-done.5
  513.4 0.0 slice-done.6
  513.4 9.1 %copy.13 = bf16[1792,7168]{1,0:T(8,128)(2,1)} copy(bf16[1792,7168]{1,0:T(8,128)(2,1)S(1)} %bitcast.1) | data formatting | bytes 51380224
  (1 shorter events, 0.0 us)
Async XLA Ops:
  485.6 27.8 %slice-start = ((s8[25690112]{0:T(1024)(128)(4,1)}), s8[4194304]{0:T(1024)(128)(4,1)S(1)}, s32[]{:S(2)}) async-start(s8[25690112]{0:T(1024)(128)(4,1)} %bitcast), calls=%async_computation | async-start | bytes 8388608
  488.9 24.4 %slice-start.1 = ((s8[25690112]{0:T(1024)(128)(4,1)}), s8[4194304]{0:T(1024)(128)(4,1)S(1)}, s32[]{:S(2)}) async-start(s8[25690112]{0:T(1024)(128)(4,1)} %bitcast), calls=%async_computation.1 | async-start | bytes 8388608
  488.9 24.4 %slice-start.2 = ((s8[25690112]{0:T(1024)(128)(4,1)}), s8[4194304]{0:T(1024)(128)(4,1)S(1)}, s32[]{:S(2)}) async-start(s8[25690112]{0:T(1024)(128)(4,1)} %bitcast), calls=%async_computation.2 | async-start | bytes 8388608
  488.9 24.4 %slice-start.3 = ((s8[25690112]{0:T(1024)(128)(4,1)}), s8[4194304]{0:T(1024)(128)(4,1)S(1)}, s32[]{:S(2)}) async-start(s8[25690112]{0:T(1024)(128)(4,1)} %bitcast), calls=%async_computation.3 | async-start | bytes 8388608
  488.9 24.4 %slice-start.4 = ((s8[25690112]{0:T(1024)(128)(4,1)}), s8[4194304]{0:T(1024)(128)(4,1)S(1)}, s32[]{:S(2)}) async-start(s8[25690112]{0:T(1024)(128)(4,1)} %bitcast), calls=%async_computation.4 | async-start | bytes 8388608
  488.9 24.4 %slice-start.5 = ((s8[25690112]{0:T(1024)(128)(4,1)}), s8[4194304]{0:T(1024)(128)(4,1)S(1)}, s32[]{:S(2)}) async-start(s8[25690112]{0:T(1024)(128)(4,1)} %bitcast), calls=%async_computation.5 | async-start | bytes 8388608
  488.9 24.4 %slice-start.6 = ((s8[25690112]{0:T(1024)(128)(4,1)}), s8[524288]{0:T(1024)(128)(4,1)S(1)}, s32[]{:S(2)}) async-start(s8[25690112]{0:T(1024)(128)(4,1)} %bitcast), calls=%async_computation.6 | async-start | bytes 1048576

commit v4 on v3

--- a/solution.py
+++ b/solution.py
@@ -11,12 +11,15 @@
 NY, NZ, NC = 2, 4, 2
 RING = 4
 OWN = 6
+DRING = 3
 WINDOW = 2
 TAIL = 4
 SLACK = 12.0
 LEAD = 5
 ROOT = 0.7978845608028654
 CUBE = 0.044715
+END = NZ - 1
+ROW_BY_ROW = (((1,), (1,)), ((), ()))
 
 
 def relays(inner, n):
@@ -54,10 +57,10 @@
 def bwd_kernel(
     dims,
     x_ref, dy_ref, pre_ref, win_ref, wdn_ref,
-    dx_ref, dwin_ref, dwdn_ref, fx_ref, fdy_ref,
-    dpre, hidt, in_r, in_l, in_d, in_y, in_w, in_e,
-    rz, ry, rd, szp, szm, sy, sd, rx, sx, lsem, ls1, ls2,
-    r_r, r_l, r_d, r_y, r_w, r_e, s_r, s_l, s_d, s_y, s_w, s_e,
+    dx_ref, dwin_ref, dwdn_ref, fx_ref, fdy_ref, fe_ref,
+    dpre, hidt, in_r, in_l, in_d, in_y,
+    rz, ry, rd, szp, szm, sy, sd, rx, sx, lsem, ls1, ls2, ls3,
+    r_r, r_l, r_d, r_y, r_ed, r_ez, s_r, s_l, s_d, s_y, s_ed, s_ez,
     rxz, sxz, rxy, sxy, rxd, sxd, cred,
 ):
     rows, d, ff, tn, nch, fn = dims
@@ -69,10 +72,11 @@
     z = (t // NC) % NZ
     y = t // (NC * NZ)
     yz = y * NZ + z
+    other_y, other_c = 1 - y, 1 - c
     p_zp, p_zm = t + NC, t - NC
-    p_y = ((1 - y) * NZ + z) * NC + c
-    p_d = yz * NC + (1 - c)
-    first, last = z == 0, z == NZ - 1
+    p_y = (other_y * NZ + z) * NC + c
+    p_d = yz * NC + other_c
+    first, last = z == 0, z == END
 
     def remote(src, dst, ssem, rsem, to):
         return pltpu.make_async_remote_copy(
@@ -145,9 +149,9 @@
         def _():
             do(lambda i: xz(i, away, 0, 1, 2))
 
-        @pl.when(z == NZ - 1 - end)
-        def _():
-            do(lambda i: xz(i, away, 0, 0 if away == 1 else NZ - 1))
+        @pl.when(z == END - end)
+        def _():
+            do(lambda i: xz(i, away, 0, 0 if away == 1 else END))
 
     def move_x(s):
         @pl.when(inside(s))
@@ -174,8 +178,8 @@
 
             @pl.when(z == 1)
             def _():
-                xz(j, -1, 0, NZ - 1).wait_recv()
-                send(j, lambda i: xz(i, -1, 1, NZ - 1))
+                xz(j, -1, 0, END).wait_recv()
+                send(j, lambda i: xz(i, -1, 1, END))
 
         @pl.when(inside(s - 4))
         def _():
@@ -187,13 +191,13 @@
 
             @pl.when(first)
             def _():
-                xz(j, -1, 1, NZ - 1).wait_recv()
+                xz(j, -1, 1, END).wait_recv()
 
             send(j, lambda i: xy(i, y))
 
         @pl.when(inside(s - 6))
         def _():
-            xy(s - 6, 1 - y).wait_recv()
+            xy(s - 6, other_y).wait_recv()
             send(s - 6, lambda i: xd(i, c))
 
     def step_in():
@@ -219,6 +223,60 @@
         @pl.when(jnp.logical_not(first))
         def _():
             signal(cred.at[0], p_zm)
+
+    nearly = (nt + 1) // 2
+    nxt = jnp.where(first, 1, NZ - 2)
+    p_nxt = jnp.where(first, p_zp, p_zm)
+
+    def edcopy(out, r):
+        return remote(out.at[r % 2], in_d.at[r % DRING, pl.ds(0, NY)], s_ed.at[r % 2], r_ed.at[r % DRING], p_d)
+
+    def ezcopy(r, out=None):
+        src = fe_ref.at[r] if out is None else out.at[r % 2]
+        return remote(src, fe_ref.at[r], s_ez.at[r % 2], r_ez.at[r], p_nxt)
+
+    def early_step(r, wte, e_d, e_own, e_out):
+        def get_w(i):
+            return pltpu.make_async_copy(win_ref.at[cols(2 * i, tn)], wte, ls3.at[0])
+
+        @pl.when((r >= 1) & (r <= nearly))
+        def _():
+            k = r - 1
+
+            @pl.when(k >= 2)
+            def _():
+                ezcopy(k - 2, e_out).wait_send()
+
+            edcopy(e_d, k).wait_recv()
+            e_out[k % 2] = (e_own[k % 2] + in_d[k % DRING, :NY].astype(F32)).astype(BF16)
+            ezcopy(k, e_out).start()
+
+        @pl.when(r == -1)
+        def _():
+            get_w(0).start()
+
+        @pl.when((r >= 0) & (r < nearly))
+        def _():
+            get_w(r).wait()
+
+            @pl.when(r >= 2)
+            def _():
+                edcopy(e_d, r - 2).wait_send()
+
+            def dot(core, h):
+                return lax.dot_general(
+                    dpre[h * NZ + nxt, core], wte[...], ROW_BY_ROW, preferred_element_type=F32
+                )
+
+            for h in range(NY):
+                e_d[r % 2, h] = dot(other_c, h).astype(BF16)
+            edcopy(e_d, r).start()
+            for h in range(NY):
+                e_own[r % 2, h] = dot(c, h)
+
+            @pl.when(r + 1 < nearly)
+            def _():
+                get_w(r + 1).start()
 
     def dy_at(b, core, q):
         return fdy_ref.at[b, core, :, cols(q, ck)]
@@ -309,11 +367,11 @@
         w_load.wait()
 
         o1 = jnp.where(z == 0, 1, z - 1)
-        o2 = jnp.where(z == NZ - 1, 1, jnp.where(z == 2, 3, 2))
+        o2 = jnp.where(z == END, 1, jnp.where(z == 2, 3, 2))
         o3 = jnp.where(z < 2, 3, 0)
 
         def pass_z(row, zb, q):
-            @pl.when((zb < z) & (z < NZ - 1))
+            @pl.when((zb < z) & (z < END))
             def _():
                 zcopy(row, zb, q, 1).start()
 
@@ -322,7 +380,7 @@
                 zcopy(row, zb, q, -1).start()
 
         def chip(i):
-            row = jnp.where((i == 0) | (i == 1) | (i == 3) | (i == 6), y, 1 - y)
+            row = jnp.where((i == 0) | (i == 1) | (i == 3) | (i == 6), y, other_y)
             near = jnp.where((i == 0) | (i == 2), z, o1)
             return row, jnp.where(i > 5, o3, jnp.where((i == 3) | (i == 5), o2, near))
 
@@ -344,15 +402,15 @@
 
             @pl.when((row != y) & (q == 0) & (i == 2))
             def _():
-                ycopy(1 - y, z, 0).wait_recv()
+                ycopy(other_y, z, 0).wait_recv()
 
                 @pl.when(jnp.logical_not(last))
                 def _():
-                    zcopy(1 - y, z, 0, 1).start()
+                    zcopy(other_y, z, 0, 1).start()
 
                 @pl.when(jnp.logical_not(first))
                 def _():
-                    zcopy(1 - y, z, 0, -1).start()
+                    zcopy(other_y, z, 0, -1).start()
 
                 @pl.when(first)
                 def _():
@@ -364,8 +422,8 @@
 
             @pl.when((row != y) & (q == 0) & (i != 2))
             def _():
-                zcopy(1 - y, zb, 0, 1).wait_recv()
-                pass_z(1 - y, zb, 0)
+                zcopy(other_y, zb, 0, 1).wait_recv()
+                pass_z(other_y, zb, 0)
 
                 @pl.when((i == 4) & (z == 1))
                 def _():
@@ -388,7 +446,7 @@
                         move_x(v)
                         step_out()
 
-                ycopy(1 - y, zb, q).wait_recv()
+                ycopy(other_y, zb, q).wait_recv()
 
             @pl.when(i > 0)
             def _():
@@ -401,9 +459,10 @@
                     move_x(v)
                     step_out()
 
-        def stream(dyc, preu, acc):
+        def stream(dyc, preu, acc, wte, e_d, e_own, e_out):
             orders = [[relays(inner_chip, nch)[e] for e in range(NY * NZ * nch)] for inner_chip in (False, True)]
             places = len(orders[0])
+            ready = 1 + max(e for e, code in enumerate(orders[0]) if code // 256 in (1, 4))
 
             def at(e):
                 code = jnp.where(inner, orders[1][0], orders[0][0])
@@ -421,7 +480,7 @@
             def fetch(code, slot):
                 i, q, _, _ = unpack(code)
                 row, zb = chip(i)
-                dcopy(row * NZ + zb, 1 - c, q).wait_recv()
+                dcopy(row * NZ + zb, other_c, q).wait_recv()
                 get(code, slot).start()
 
             def get_pre(u, keep):
@@ -452,7 +511,7 @@
                 lhs = dyc[e % 2].reshape(NC * rows, ck)
                 for n in range(0, ff, fn):
                     term = lax.dot_general(
-                        lhs, wdn[n : n + fn, cols(q, ck)], (((1,), (1,)), ((), ())), preferred_element_type=F32
+                        lhs, wdn[n : n + fn, cols(q, ck)], ROW_BY_ROW, preferred_element_type=F32
                     )
                     acc[keep, :, n : n + fn] = jnp.where(mark % 2 == 1, 0.0, acc[keep, :, n : n + fn]) + term
 
@@ -469,6 +528,10 @@
 
                     loop(ff // fn, part)
 
+                @pl.when(edge)
+                def _():
+                    early_step(e - ready, wte, e_d, e_own, e_out)
+
                 return following, later
 
             codes = at(0), at(1)
@@ -477,11 +540,21 @@
             fetch(codes[0], 0)
             lax.fori_loop(0, places, place, codes)
 
+            @pl.when(edge)
+            def _():
+                for r in range(nearly - 2, nearly):
+                    edcopy(e_d, r).wait_send()
+                    ezcopy(r, e_out).wait_send()
+
         pl.run_scoped(
             stream,
             pltpu.VMEM((2, NC, rows, ck), BF16),
             pltpu.VMEM((3, NC * rows, ff), BF16),
             pltpu.VMEM((3, NC * rows, ff), F32),
+            pltpu.VMEM((tn, ff), BF16),
+            pltpu.VMEM((2, NY, rows, tn), BF16),
+            pltpu.VMEM((2, NY, rows, tn), F32),
+            pltpu.VMEM((2, NY, rows, tn), BF16),
         )
 
     pl.run_scoped(phase1, pltpu.VMEM((ff, d), BF16))
@@ -489,7 +562,7 @@
     def all_sent():
         def sent(q):
             def block(zb):
-                @pl.when((zb <= z) & (z < NZ - 1))
+                @pl.when((zb <= z) & (z < END))
                 def _():
                     zcopy(y, zb, q, 1).wait_send()
 
@@ -499,13 +572,13 @@
 
                 @pl.when(q == 0)
                 def _():
-                    @pl.when((zb <= z) & (z < NZ - 1))
+                    @pl.when((zb <= z) & (z < END))
                     def _():
-                        zcopy(1 - y, zb, q, 1).wait_send()
+                        zcopy(other_y, zb, q, 1).wait_send()
 
                     @pl.when((zb >= z) & (z > 0))
                     def _():
-                        zcopy(1 - y, zb, q, -1).wait_send()
+                        zcopy(other_y, zb, q, -1).wait_send()
 
                 @pl.when((q > 0) | (zb == z))
                 def _():
@@ -524,7 +597,7 @@
         def _():
             xcopy(1, p_zm, yz).wait_send()
 
-    def phase2(own, out_r, out_l, out_d, out_y, out_w, out_e, wt, dyt, xt, odn, oin, odx, ls):
+    def phase2(own, out_r, out_l, out_d, out_y, ein, wt, dyt, xt, odn, oin, odx, ls):
         steps = nt + TAIL
 
         def rcopy(slot, k):
@@ -544,7 +617,7 @@
 
             @pl.when(inside(j))
             def _():
-                slot, ring = j % RING, j % OWN
+                slot, ring = j % DRING, j % OWN
                 dsum(slot).wait_recv()
 
                 def piece(b):
@@ -553,18 +626,18 @@
                 loop(NY * NZ, piece)
 
         def along(s, away, start, copy, inb, outb):
-            behind = z if away == 1 else NZ - 1 - z
+            behind = z if away == 1 else END - z
             j = s - 1 - behind
 
             @pl.when(inside(j))
             def _():
                 slot, ring = j % RING, j % OWN
-                swaps = j % 2 == 0
-                for k in range(NZ - 1, 0, -1):
+                sent = j % 2 == 0
+                for k in range(END, 0, -1):
                     zz = z + away * k
                     here = (zz >= 0) & (zz < NZ)
                     if k == 1:
-                        here = here & jnp.logical_not(start & swaps)
+                        here = here & jnp.logical_not(start & sent)
 
                     @pl.when(here)
                     def _():
@@ -579,7 +652,7 @@
 
                             loop(NY, piece)
 
-                        if k < NZ - 1:
+                        if k < END:
 
                             @pl.when(jnp.logical_not(start))
                             def _():
@@ -593,8 +666,8 @@
                         copy(slot, k - 1).start()
 
         def settle(s, away, copy, inb):
-            behind = z if away == 1 else NZ - 1 - z
-            j = s - behind - jnp.where(behind == NZ - 1, 1, 2)
+            behind = z if away == 1 else END - z
+            j = s - behind - jnp.where(behind == END, 1, 2)
 
             @pl.when(inside(j) & ((behind > 1) | ((behind == 1) & (j % 2 == 1))))
             def _():
@@ -606,46 +679,21 @@
 
                 loop(NY, piece)
 
-        nxt = jnp.where(first, 1, NZ - 2)
-        p_nxt = jnp.where(first, p_zp, p_zm)
-        p_end = jnp.where(z == 1, p_zm, p_zp)
-
-        def wcopy(slot):
-            return remote(out_w.at[slot], in_w.at[slot], s_w.at[slot], r_w.at[slot], p_y)
-
-        def ecopy(slot, to):
-            return remote(out_e.at[slot], in_e.at[slot], s_e.at[slot], r_e.at[slot], to)
-
-        def swap(s):
-            def at(j, where, body):
-                @pl.when(inside(j) & (j % 2 == 0) & where)
-                def _():
-                    body(j % RING, j % OWN, j >= RING)
-
-            def give(slot, ring, again):
-                @pl.when(again)
-                def _():
-                    wcopy(slot).wait_send()
-
-                out_w[slot] = own[ring, 1 - y, nxt].astype(BF16)
-                wcopy(slot).start()
-
-            def join(slot, ring, again):
-                @pl.when(again)
-                def _():
-                    ecopy(slot, p_nxt).wait_send()
-
-                wcopy(slot).wait_recv()
-                out_e[slot] = (own[ring, y, nxt] + in_w[slot].astype(F32)).astype(BF16)
-                ecopy(slot, p_nxt).start()
-
-            def take(slot, ring, again):
-                ecopy(slot, p_end).wait_recv()
-                own[ring, y, z] += in_e[slot].astype(F32)
-
-            at(s - 1, edge, give)
-            at(s - 3, edge, join)
-            at(s - 4, inner, take)
+        def get_early(r):
+            return pltpu.make_async_copy(fe_ref.at[r], ein.at[r % 2], ls.at[6, r % 2])
+
+        def take_early(s):
+            @pl.when(inner & (s % 2 == 0) & inside(s - 4))
+            def _():
+                r, ring = (s - 4) // 2, (s - 4) % OWN
+                get_early(r).wait()
+                own[ring, :, z] += ein[r % 2].astype(F32)
+
+            @pl.when(inner & (s % 2 == 0) & inside(s - 2))
+            def _():
+                r = (s - 2) // 2
+                ezcopy(r).wait_recv()
+                get_early(r).start()
 
         def across(s):
             j = s - 4
@@ -658,7 +706,7 @@
                 def _():
                     ysum(slot).wait_send()
 
-                out_y[slot] = own[ring, 1 - y, z].astype(BF16)
+                out_y[slot] = own[ring, other_y, z].astype(BF16)
                 ysum(slot).start()
 
         def put_dx(j):
@@ -695,25 +743,25 @@
             return pltpu.make_async_copy(oin.at[j % 2], dwin_ref.at[cols(j, tn)], ls.at[4, j % 2])
 
         def term(j):
-            slot, ring = j % RING, j % OWN
+            slot, ring = j % DRING, j % OWN
             get_w(j).wait()
 
             @pl.when(j + 1 < nt)
             def _():
                 get_w(j + 1).start()
 
-            @pl.when(j >= RING)
+            @pl.when(j >= DRING)
             def _():
                 dsum(slot).wait_send()
 
             def dot(core, h):
                 lhs = dpre[h * NZ : (h + 1) * NZ, core].reshape(NZ * rows, ff)
                 return lax.dot_general(
-                    lhs, wt[j % 2], (((1,), (1,)), ((), ())), preferred_element_type=F32
+                    lhs, wt[j % 2], ROW_BY_ROW, preferred_element_type=F32
                 ).reshape(NZ, rows, tn)
 
             for h in range(NY):
-                out_d[slot, h * NZ : (h + 1) * NZ] = dot(1 - c, h).astype(BF16)
+                out_d[slot, h * NZ : (h + 1) * NZ] = dot(other_c, h).astype(BF16)
             dsum(slot).start()
             for h in range(NY):
                 own[ring, h] = dot(c, h)
@@ -761,11 +809,11 @@
         def step(s):
             step_in()
             add_core(s)
-            swap(s)
             along(s, 1, first, rcopy, in_r, out_r)
             along(s, -1, last, lcopy, in_l, out_l)
             settle(s, 1, rcopy, in_r)
             settle(s, -1, lcopy, in_l)
+            take_early(s)
             across(s)
             finish(s)
             move_x(s + LEAD)
@@ -784,7 +832,7 @@
 
             @pl.when(inside(s - 1))
             def _():
-                xd(s - 1, 1 - c).wait_recv()
+                xd(s - 1, other_c).wait_recv()
                 get_x(s - 1).start()
 
             m = s - s // 9 - 1
@@ -802,25 +850,17 @@
 
         for j in range(nt - RING, nt):
             slot = j % RING
-            for k in range(NZ - 1):
-                swapped = k == 0 and j % 2 == 0
-
-                @pl.when((z + k + 1 < NZ) & jnp.logical_not(first & swapped))
+            for k in range(END):
+                early = k == 0 and j % 2 == 0
+
+                @pl.when((z + k + 1 < NZ) & jnp.logical_not(first & early))
                 def _():
                     rcopy(slot, k).wait_send()
 
-                @pl.when((z - k - 1 >= 0) & jnp.logical_not(last & swapped))
+                @pl.when((z - k - 1 >= 0) & jnp.logical_not(last & early))
                 def _():
                     lcopy(slot, k).wait_send()
 
-            if j % 2 == 0:
-
-                @pl.when(edge)
-                def _():
-                    wcopy(slot).wait_send()
-                    ecopy(slot, p_nxt).wait_send()
-
-            dsum(slot).wait_send()
             ysum(slot).wait_send()
             xy(j, y).wait_send()
             xd(j, c).wait_send()
@@ -833,7 +873,10 @@
 
             @pl.when(z == 1)
             def _():
-                xz(j, -1, 1, NZ - 1).wait_send()
+                xz(j, -1, 1, END).wait_send()
+
+        for j in range(nt - DRING, nt):
+            dsum(j % DRING).wait_send()
 
         for j in range(nt - 2, nt):
             put_dn(j).wait()
@@ -843,19 +886,18 @@
     pl.run_scoped(
         phase2,
         pltpu.VMEM((OWN, NY, NZ, rows, tn), F32),
-        pltpu.VMEM((RING, NZ - 1, NY, rows, tn), BF16),
-        pltpu.VMEM((RING, NZ - 1, NY, rows, tn), BF16),
-        pltpu.VMEM((RING, NY * NZ, rows, tn), BF16),
+        pltpu.VMEM((RING, END, NY, rows, tn), BF16),
+        pltpu.VMEM((RING, END, NY, rows, tn), BF16),
+        pltpu.VMEM((DRING, NY * NZ, rows, tn), BF16),
         pltpu.VMEM((RING, rows, tn), BF16),
-        pltpu.VMEM((RING, rows, tn), BF16),
-        pltpu.VMEM((RING, rows, tn), BF16),
+        pltpu.VMEM((2, NY, rows, tn), BF16),
         pltpu.VMEM((2, tn, ff), BF16),
         pltpu.VMEM((2, NY * NZ, NC, rows, tn), BF16),
         pltpu.VMEM((2, NY * NZ, NC, rows, tn), BF16),
         pltpu.VMEM((2, ff, tn), BF16),
         pltpu.VMEM((2, tn, ff), BF16),
         pltpu.VMEM((2, rows, tn), BF16),
-        pltpu.SemaphoreType.DMA((6, 2)),
+        pltpu.SemaphoreType.DMA((7, 2)),
     )
 
 
@@ -863,6 +905,7 @@
     blocks = NY * NZ
     total = blocks * NC * rows
     dma = pltpu.SemaphoreType.DMA
+    early = (d // tn + 1) // 2
     any_ = pl.BlockSpec(memory_space=pl.ANY)
     return pl.pallas_call(
         functools.partial(bwd_kernel, (rows, d, ff, tn, nch, fn)),
@@ -873,23 +916,22 @@
             jax.ShapeDtypeStruct((ff, d), BF16),
             jax.ShapeDtypeStruct((blocks, NC, rows, d), BF16),
             jax.ShapeDtypeStruct((blocks, NC, rows, d), BF16),
+            jax.ShapeDtypeStruct((early, NY, rows, tn), BF16),
         ],
         in_specs=[any_] * 5,
-        out_specs=[any_] * 5,
+        out_specs=[any_] * 6,
         scratch_shapes=[
             pltpu.VMEM((blocks, NC, rows, ff), BF16),
             pltpu.VMEM((ff, total), BF16),
-            pltpu.VMEM((RING, NZ - 1, NY, rows, tn), BF16),
-            pltpu.VMEM((RING, NZ - 1, NY, rows, tn), BF16),
-            pltpu.VMEM((RING, blocks, rows, tn), BF16),
-            pltpu.VMEM((RING, rows, tn), BF16),
-            pltpu.VMEM((RING, rows, tn), BF16),
+            pltpu.VMEM((RING, END, NY, rows, tn), BF16),
+            pltpu.VMEM((RING, END, NY, rows, tn), BF16),
+            pltpu.VMEM((DRING, blocks, rows, tn), BF16),
             pltpu.VMEM((RING, rows, tn), BF16),
             dma((NZ, nch + 1)), dma((NZ, nch)), dma((blocks, nch)),
             dma((NZ, nch + 1)), dma((NZ, nch + 1)), dma((NZ, nch)), dma((blocks, nch)),
-            dma((2,)), dma((2,)), dma((3,)), dma((2,)), dma((3,)),
-            dma((RING, NZ - 1)), dma((RING, NZ - 1)), dma((RING,)), dma((RING,)), dma((RING,)), dma((RING,)),
-            dma((RING, NZ - 1)), dma((RING, NZ - 1)), dma((RING,)), dma((RING,)), dma((RING,)), dma((RING,)),
+            dma((2,)), dma((2,)), dma((3,)), dma((2,)), dma((3,)), dma((1,)),
+            dma((RING, END)), dma((RING, END)), dma((DRING,)), dma((RING,)), dma((DRING,)), dma((early,)),
+            dma((RING, END)), dma((RING, END)), dma((DRING,)), dma((RING,)), dma((2,)), dma((2,)),
             dma((2, 2, RING)), dma((2, 2, RING)), dma((RING,)), dma((RING,)), dma((RING,)), dma((RING,)),
             pltpu.SemaphoreType.REGULAR((4,)),
         ],
@@ -906,7 +948,7 @@
     def local(x, dy, pre, win, wdn):
         rows, d = x.shape
         ff = pre.shape[1]
-        dx, dwin, dwdn, _, _ = call(rows, d, ff, 256, 7, 256, x, dy, pre, win, wdn)
+        dx, dwin, dwdn = call(rows, d, ff, 256, 7, 256, x, dy, pre, win, wdn)[:3]
         return dx, dwin, dwdn
 
     return jax.shard_map(

time: 524 us -> 508 us (0.969)
  Pallas kernels: 485 us -> 470 us
    pallas_call x1, Pallas kernels: 485 us -> 470 us  [call(): pl.pallas_call(functools.partial(bwd_kernel, (rows, d, ff, tn, nch, fn)),...]
where the time goes in v4:
time: 508 us; the launch traced here: 507 us
  Pallas kernels  470 us (93%)
  local copies, waits for them, and re-layouts  36.8 us (7%)
    pallas_call x1, Pallas kernels, call(): pl.pallas_call(functools.partial(bwd_kernel, (rows, d, ff, tn, nch, fn)),...  470 us
    unnamed x17, local copies, waits for them, and re-layouts  36.8 us

profile of v4, /device:TPU:0, one launch (start us, length us, event | category | flops | bytes accessed | tf_op | source)
XLA Modules:
  0.0 507.5 jit_solution(12176916364664221581)
XLA Ops:
  0.6 469.9 %bwd.1 = (bf16[160,7168]{1,0:T(8,128)(2,1)}, bf16[7168,1792]{1,0:T(8,128)(2,1)}, bf16[1792,7168]{1,0:T(8,128)(2,1)}, bf16[8,2,160,7168]{3,2,1,0:T(8,128)(2,1)}, ...) custom-call(bf16[160,7168]{1,0:T(8,128)(2,1)} %x_ref.1, bf16[160,7168]{1,0:T(8,128)(2,1)} %dy_ref.1, ...), custom_call_target="tpu_custom_call" | custom-call | tf_op jit(solution)/shard_map/bwd/pallas_call | solution.py:910
  470.6 0.0 slice-start
  470.6 3.3 copy.11
  473.9 0.0 slice-start.1
  473.9 0.0 slice-start.2
  473.9 0.0 slice-start.3
  473.9 0.0 slice-start.4
  473.9 0.0 slice-start.5
  473.9 0.0 slice-start.6
  473.9 24.4 %copy.12 = bf16[7168,1792]{1,0:T(8,128)(2,1)} copy(bf16[7168,1792]{1,0:T(8,128)(2,1)} %get-tuple-element.13) | data formatting | bytes 51380224
  498.3 0.0 slice-done
  498.3 0.0 slice-done.1
  498.3 0.0 slice-done.2
  498.3 0.0 slice-done.3
  498.3 0.0 slice-done.4
  498.4 0.0 slice-done.5
  498.4 0.0 slice-done.6
  498.4 9.1 %copy.13 = bf16[1792,7168]{1,0:T(8,128)(2,1)} copy(bf16[1792,7168]{1,0:T(8,128)(2,1)S(1)} %bitcast.1) | data formatting | bytes 51380224
  (1 shorter events, 0.0 us)
Async XLA Ops:
  470.6 27.8 %slice-start = ((s8[25690112]{0:T(1024)(128)(4,1)}), s8[4194304]{0:T(1024)(128)(4,1)S(1)}, s32[]{:S(2)}) async-start(s8[25690112]{0:T(1024)(128)(4,1)} %bitcast), calls=%async_computation | async-start | bytes 8388608
  473.9 24.4 %slice-start.1 = ((s8[25690112]{0:T(1024)(128)(4,1)}), s8[4194304]{0:T(1024)(128)(4,1)S(1)}, s32[]{:S(2)}) async-start(s8[25690112]{0:T(1024)(128)(4,1)} %bitcast), calls=%async_computation.1 | async-start | bytes 8388608
  473.9 24.4 %slice-start.2 = ((s8[25690112]{0:T(1024)(128)(4,1)}), s8[4194304]{0:T(1024)(128)(4,1)S(1)}, s32[]{:S(2)}) async-start(s8[25690112]{0:T(1024)(128)(4,1)} %bitcast), calls=%async_computation.2 | async-start | bytes 8388608
  473.9 24.4 %slice-start.3 = ((s8[25690112]{0:T(1024)(128)(4,1)}), s8[4194304]{0:T(1024)(128)(4,1)S(1)}, s32[]{:S(2)}) async-start(s8[25690112]{0:T(1024)(128)(4,1)} %bitcast), calls=%async_computation.3 | async-start | bytes 8388608
  473.9 24.4 %slice-start.4 = ((s8[25690112]{0:T(1024)(128)(4,1)}), s8[4194304]{0:T(1024)(128)(4,1)S(1)}, s32[]{:S(2)}) async-start(s8[25690112]{0:T(1024)(128)(4,1)} %bitcast), calls=%async_computation.4 | async-start | bytes 8388608
  473.9 24.4 %slice-start.5 = ((s8[25690112]{0:T(1024)(128)(4,1)}), s8[4194304]{0:T(1024)(128)(4,1)S(1)}, s32[]{:S(2)}) async-start(s8[25690112]{0:T(1024)(128)(4,1)} %bitcast), calls=%async_computation.5 | async-start | bytes 8388608
  473.9 24.4 %slice-start.6 = ((s8[25690112]{0:T(1024)(128)(4,1)}), s8[524288]{0:T(1024)(128)(4,1)S(1)}, s32[]{:S(2)}) async-start(s8[25690112]{0:T(1024)(128)(4,1)} %bitcast), calls=%async_computation.6 | async-start | bytes 1048576
